TPU v7x, 512 devices: a whole 4x8x8 slice. The times are simulated.
512 devices in a mesh: depth: 16 (over z, y_lo), rows: 32 (over x, y_hi, core).
Axes of the slice: x: 4, y: 8 (y_hi: 4, y_lo: 2; y = y_hi * 2 + y_lo), z: 8, core: 2. Of those that a mesh axis runs over, the one named last changes fastest.
Arguments:
- target: float32 [16, 2, 4096, 4096], P('depth', None, 'rows'), may hold values from -6 to 6
- depth_index: int32 [16], P('depth'), may hold values from 0 to 255
- band_mask: int32 [16, 2, 4096], P('depth'), may hold values from 0 to 1, as said below
Outputs:
- hologram: float32 [2, 4096, 4096], P(None, ('depth', 'rows'))
Inputs may be any that keep to these rules, and one draw needn't show every extreme that they name: `band_mask`: for each plane and each of the two dimensions, the ones are exactly the frequency indices k with min(k, 4096 - k) below a cutoff between 512 and 2048.
All inputs are finite; a program needn't handle non-finite values.
Results may differ from a plain program's by a relative error of at most 0.0009.
Values sent between devices are 32-bit elements; how exact they have to be, the bound alone decides.
No kernel may reach another device: no remote copies, remote signals or barrier semaphores. Data moves between devices by JAX's collectives and lax.ppermute only.
A program may use at most 64 MiB of HBM per device.

v0:
```python
import functools
import math

import jax
import jax.numpy as jnp
import numpy as np
from jax import lax
from jax.experimental import pallas as pl
from jax.experimental.pallas import tpu as pltpu
from jax.sharding import Mesh
from jax.sharding import PartitionSpec as P

LOW = 32
HIGH = 128
N = 4096
DEPTH = ("depth_0", "depth_1")
DEPTH_ROWS = ("depth_0", "depth_1", "rows")
CHUNKS = 2
KC = HIGH // CHUNKS


def block_table(direction, scaling):
    index = np.arange(HIGH)
    angles = direction * 2.0 * np.pi / HIGH * (index[:, None] * index[None, :] % HIGH)
    cosine, sine = np.cos(angles) * scaling, np.sin(angles) * scaling
    table = np.concatenate(
        [np.concatenate([cosine, sine], 1), np.concatenate([-sine, cosine], 1)], 0
    ).astype(np.float32)
    high = table.astype(jnp.bfloat16)
    low = (table - high.astype(np.float32)).astype(jnp.bfloat16)
    return high, low


def twiddles(direction):
    product = np.arange(LOW)[:, None] * np.arange(HIGH)[None, :] % N
    angles = direction * 2.0 * np.pi / N * product
    return np.stack([np.cos(angles), np.sin(angles)]).astype(np.float32)


def add(a, b):
    return (a[0] + b[0], a[1] + b[1])


def sub(a, b):
    return (a[0] - b[0], a[1] - b[1])


def quarter(a, sign):
    return (-a[1], a[0]) if sign > 0 else (a[1], -a[0])


def turn(a, numerator, length, sign):
    numerator %= length
    if numerator == 0:
        return a
    if numerator * 4 == length:
        return quarter(a, sign)
    if numerator * 2 == length:
        return (-a[0], -a[1])
    if numerator * 8 == length:
        half = np.float32(math.sqrt(0.5))
        b = quarter(a, sign)
        return ((a[0] + b[0]) * half, (a[1] + b[1]) * half)
    if numerator * 8 == 3 * length:
        half = np.float32(math.sqrt(0.5))
        b = quarter(a, sign)
        return ((b[0] - a[0]) * half, (b[1] - a[1]) * half)
    angle = sign * 2.0 * math.pi * numerator / length
    cosine, sine = np.float32(math.cos(angle)), np.float32(math.sin(angle))
    return (a[0] * cosine - a[1] * sine, a[0] * sine + a[1] * cosine)


def four_points(values, sign):
    even, odd = add(values[0], values[2]), sub(values[0], values[2])
    even_2, odd_2 = add(values[1], values[3]), quarter(sub(values[1], values[3]), sign)
    return [add(even, even_2), add(odd, odd_2), sub(even, even_2), sub(odd, odd_2)]


def eight_points(values, sign):
    first = four_points(values[0::2], sign)
    second = four_points(values[1::2], sign)
    second = [turn(second[k], k, 8, sign) for k in range(4)]
    return [add(first[k], second[k]) for k in range(4)] + [
        sub(first[k], second[k]) for k in range(4)
    ]


def low_transform(load, store, part_ref, sign):
    for a in range(8):
        outs = four_points([load(a + 8 * b) for b in range(4)], sign)
        for q in range(4):
            pair = turn(outs[q], a * q, 32, sign)
            part_ref[q * 8 + a, 0] = pair[0]
            part_ref[q * 8 + a, 1] = pair[1]
    for q in range(4):
        values = [(part_ref[q * 8 + a, 0], part_ref[q * 8 + a, 1]) for a in range(8)]
        outs = eight_points(values, sign)
        for p in range(8):
            store(q + 4 * p, outs[p])


def product(rows, table):
    high_table, low_table = table[0][...], table[1][...]
    high = rows.astype(jnp.bfloat16)
    low = (rows - high.astype(jnp.float32)).astype(jnp.bfloat16)
    dot = functools.partial(jnp.dot, preferred_element_type=jnp.float32)
    return dot(high, high_table) + (dot(low, high_table) + dot(high, low_table))


WIDTH_ROWS = 16
WIDTH_STEPS = HIGH // WIDTH_ROWS
WIDTH_LOWS = LOW // WIDTH_STEPS


def width_kernel(x_ref, tw_ref, high_ref, low_ref, *rest):
    out_refs, (mid_ref, part_ref) = rest[:CHUNKS], rest[CHUNKS:]
    step = pl.program_id(0)

    @pl.when(step < WIDTH_STEPS)
    def _():
        for g in range(WIDTH_ROWS // 8):
            rows = pl.ds(pl.multiple_of(step * WIDTH_ROWS + 8 * g, 8), 8)

            def load(n):
                lanes = slice(HIGH * n, HIGH * (n + 1))
                return (
                    x_ref[0, 0, 8 * g : 8 * g + 8, lanes],
                    x_ref[0, 1, 8 * g : 8 * g + 8, lanes],
                )

            def store(k, pair):
                cosine, sine = tw_ref[0, k : k + 1, :], tw_ref[1, k : k + 1, :]
                mid_ref[k, rows, 0:HIGH] = pair[0] * cosine - pair[1] * sine
                mid_ref[k, rows, HIGH:] = pair[0] * sine + pair[1] * cosine

            low_transform(load, store, part_ref.at[g], -1)

    @pl.when(step >= WIDTH_STEPS)
    def _():
        base = (step - WIDTH_STEPS) * WIDTH_LOWS
        for k in range(WIDTH_LOWS):
            done = product(mid_ref[base + k], (high_ref, low_ref))
            for c in range(2):
                flat = done[:, HIGH * c : HIGH * (c + 1)].T
                for i in range(CHUNKS):
                    out_refs[i][k, c] = flat[KC * i : KC * (i + 1)]


def whole(*dims):
    return pl.BlockSpec(dims, lambda i: (0,) * len(dims))


def along_width(target):
    high, low = block_table(-1.0, 1.0 / 64)
    shape = jax.ShapeDtypeStruct((LOW, 2, KC, HIGH), jnp.float32)
    spec = pl.BlockSpec(
        (WIDTH_LOWS, 2, KC, HIGH), lambda i: (jnp.maximum(i - WIDTH_STEPS, 0), 0, 0, 0)
    )
    return pl.pallas_call(
        width_kernel,
        name="along_width",
        grid=(2 * WIDTH_STEPS,),
        in_specs=[
            pl.BlockSpec(
                (1, 2, WIDTH_ROWS, N), lambda i: (0, 0, jnp.minimum(i, WIDTH_STEPS - 1), 0)
            ),
            whole(2, LOW, HIGH),
            whole(2 * HIGH, 2 * HIGH),
            whole(2 * HIGH, 2 * HIGH),
        ],
        out_specs=[spec] * CHUNKS,
        out_shape=[shape] * CHUNKS,
        scratch_shapes=[
            pltpu.VMEM((LOW, HIGH, 2 * HIGH), jnp.float32),
            pltpu.VMEM((WIDTH_ROWS // 8, LOW, 2, 8, HIGH), jnp.float32),
        ],
        cost_estimate=pl.CostEstimate(
            flops=6 * N * 512 * 256, bytes_accessed=8 << 20, transcendentals=0
        ),
    )(target, jnp.asarray(twiddles(-1.0)), jnp.asarray(high), jnp.asarray(low))


HEIGHT_ROWS = 16


def height_kernel(x_ref, h_ref, ftw_ref, fh_ref, fl_ref, btw_ref, bh_ref, bl_ref,
                  out_ref, mid_ref, part_ref):
    groups = HEIGHT_ROWS // 8
    for g in range(groups):
        rows = slice(8 * g, 8 * g + 8)

        def load(n):
            return (x_ref[n, 0, rows, :], x_ref[n, 1, rows, :])

        def store(k, pair):
            cosine, sine = ftw_ref[0, k : k + 1, :], ftw_ref[1, k : k + 1, :]
            mid_ref[k, rows, 0:HIGH] = pair[0] * cosine - pair[1] * sine
            mid_ref[k, rows, HIGH:] = pair[0] * sine + pair[1] * cosine

        low_transform(load, store, part_ref.at[g], -1)

    count = 8
    for b in range(0, LOW, count):
        part = slice(b, b + count)
        flat = mid_ref[part].reshape(count * HEIGHT_ROWS, 2 * HIGH)
        spectrum = product(flat, (fh_ref, fl_ref))
        real, imaginary = spectrum[:, :HIGH], spectrum[:, HIGH:]
        cosine = h_ref[part, 0].reshape(count * HEIGHT_ROWS, HIGH)
        sine = h_ref[part, 1].reshape(count * HEIGHT_ROWS, HIGH)
        moved = jnp.concatenate(
            [real * cosine - imaginary * sine, real * sine + imaginary * cosine], axis=1
        )
        back = product(moved, (bh_ref, bl_ref))
        mid_ref[part] = back.reshape(count, HEIGHT_ROWS, 2 * HIGH)

    for g in range(groups):
        rows = slice(8 * g, 8 * g + 8)

        def load(k):
            real, imaginary = mid_ref[k, rows, 0:HIGH], mid_ref[k, rows, HIGH:]
            cosine, sine = btw_ref[0, k : k + 1, :], btw_ref[1, k : k + 1, :]
            return (real * cosine - imaginary * sine, real * sine + imaginary * cosine)

        def store(n, pair):
            out_ref[n, 0, rows, :] = pair[0]
            out_ref[n, 1, rows, :] = pair[1]

        low_transform(load, store, part_ref.at[g], 1)


def along_height(columns, transfer):
    spec = pl.BlockSpec((LOW, 2, HEIGHT_ROWS, HIGH), lambda i: (0, 0, i, 0))
    table = whole(2 * HIGH, 2 * HIGH)
    forward, backward = block_table(-1.0, 1.0 / 64), block_table(1.0, 1.0 / 64)
    count = columns.shape[2]
    return pl.pallas_call(
        height_kernel,
        name="along_height",
        grid=(count // HEIGHT_ROWS,),
        in_specs=[spec, spec, whole(2, LOW, HIGH), table, table, whole(2, LOW, HIGH), table, table],
        out_specs=spec,
        out_shape=jax.ShapeDtypeStruct((LOW, 2, count, HIGH), jnp.float32),
        scratch_shapes=[
            pltpu.VMEM((LOW, HEIGHT_ROWS, 2 * HIGH), jnp.float32),
            pltpu.VMEM((HEIGHT_ROWS // 8, LOW, 2, 8, HIGH), jnp.float32),
        ],
        cost_estimate=pl.CostEstimate(
            flops=12 * LOW * count * 512 * 256,
            bytes_accessed=3 * 8 * LOW * count * HIGH,
            transcendentals=0,
        ),
    )(
        columns,
        transfer,
        jnp.asarray(twiddles(-1.0)),
        *[jnp.asarray(t) for t in forward],
        jnp.asarray(twiddles(1.0)),
        *[jnp.asarray(t) for t in backward],
    )


def flip_kernel(*refs):
    in_refs, out_ref = refs[:-1], refs[-1]
    for n in range(out_ref.shape[0] // 16):
        for c in range(2):
            whole_tile = jnp.concatenate([ref[n, c] for ref in in_refs], axis=0)
            out_ref[16 * n : 16 * n + 16, c] = whole_tile.T.reshape(16, 8, HIGH)


def flip(shares):
    count = 16 * shares[0].shape[0]
    return pl.pallas_call(
        flip_kernel,
        name="flip",
        out_shape=jax.ShapeDtypeStruct((count, 2, 8, HIGH), jnp.float32),
    )(*shares)


def inverse_width_kernel(x_ref, tw_ref, high_ref, low_ref, out_ref, mid_ref, part_ref):
    total = x_ref[0:LOW] + x_ref[LOW:]
    rows = jnp.concatenate([total[:, 0], total[:, 1]], axis=-1).reshape(LOW * 8, 2 * HIGH)
    mid_ref[...] = product(rows, (high_ref, low_ref)).reshape(LOW, 8, 2 * HIGH)

    def load(k):
        real, imaginary = mid_ref[k, :, 0:HIGH], mid_ref[k, :, HIGH:]
        cosine, sine = tw_ref[0, k : k + 1, :], tw_ref[1, k : k + 1, :]
        return (real * cosine - imaginary * sine, real * sine + imaginary * cosine)

    def store(n, pair):
        out_ref[0, :, HIGH * n : HIGH * (n + 1)] = pair[0]
        out_ref[1, :, HIGH * n : HIGH * (n + 1)] = pair[1]

    low_transform(load, store, part_ref, 1)


def inverse_width(pieces, scaling):
    high, low = block_table(1.0, scaling / 64)
    return pl.pallas_call(
        inverse_width_kernel,
        name="inverse_width",
        out_shape=jax.ShapeDtypeStruct((2, 8, N), jnp.float32),
        scratch_shapes=[
            pltpu.VMEM((LOW, 8, 2 * HIGH), jnp.float32),
            pltpu.VMEM((LOW, 2, 8, HIGH), jnp.float32),
        ],
    )(pieces, jnp.asarray(twiddles(1.0)), jnp.asarray(high), jnp.asarray(low))


def signed(natural):
    return jnp.where(natural < N // 2, natural, natural - N)


def transfer_factors(depth_index, band_mask, column):
    high = jnp.arange(HIGH, dtype=jnp.int32)
    low = jnp.arange(LOW, dtype=jnp.int32)
    height = signed(low[:, None] + LOW * high[None, :])
    width = signed(column + LOW * high)
    square = (height * height)[:, None, :] + (width * width)[None, :, None]
    square = square.astype(jnp.float32) * np.float32(1.0 / (N * N))
    descent = -square / (jnp.sqrt(4.0 - square) + 2.0)
    turns = (100.0 + 2.0 * depth_index[0].astype(jnp.float32)) * descent
    angles = np.float32(2.0 * math.pi) * (turns - jnp.round(turns))
    mask_height = band_mask[0, 0].reshape(HIGH, LOW).T.astype(jnp.float32)
    mask_width = lax.dynamic_slice_in_dim(
        band_mask[0, 1].reshape(HIGH, LOW).T, column, 1, 0
    )[0].astype(jnp.float32)
    weights = mask_height[:, None, :] * mask_width[None, :, None]
    return jnp.stack([jnp.cos(angles) * weights, jnp.sin(angles) * weights], axis=1)


def local(target, depth_index, band_mask):
    spectra = along_width(target)
    transfer = transfer_factors(depth_index, band_mask, lax.axis_index("rows"))
    shares = []
    for i in range(CHUNKS):
        columns = lax.all_to_all(spectra[i], "rows", split_axis=0, concat_axis=0, tiled=True)
        part = along_height(columns, transfer[:, :, KC * i : KC * (i + 1)])
        shares.append(lax.psum_scatter(part, "depth_0", scatter_dimension=0, tiled=True))
    pieces = lax.all_to_all(
        flip(shares), ("depth_1", "rows"), split_axis=0, concat_axis=0, tiled=True
    )
    return inverse_width(pieces, 1.0 / math.sqrt(lax.axis_size(DEPTH)))


def solution(mesh):
    split = Mesh(mesh.devices.reshape(8, 2, mesh.shape["rows"]), ("depth_0", "depth_1", "rows"))
    in_specs = (P(DEPTH, None, "rows", None), P(DEPTH), P(DEPTH, None, None))
    out_specs = P(None, DEPTH_ROWS, None)
    return jax.shard_map(local, mesh=split, in_specs=in_specs, out_specs=out_specs, check_vma=False)
```

profile of v0, /device:TPU:1, one launch (start us, length us, event | category | flops | bytes accessed | tf_op | source)
XLA Modules:
  0.0 231.2 jit_solution(13349622797447209914)
XLA Ops:
  6.5 11.2 %along_width.1 = (f32[32,2,64,128]{3,2,1,0:T(8,128)}, f32[32,2,64,128]{3,2,1,0:T(8,128)}) custom-call(f32[1,2,128,4096]{3,2,1,0:T(8,128)} %x_ref.1, f32[2,32,128]{2,1,0:T(8,128)} %constant.48.clone.tw_ref.ftw_ref, bf16[256,256]{1,0:T(8,128)(2,1)} %constant.49.clone.high_ref.fh_ref, bf16[256,256]{1,0:T(8,128)(2,1)} %constant.50.clone.low_ref.fl_ref), custom_call_target="tpu_custom_call" | custom-call | flops 3221225472 | bytes 8388608 | tf_op jit(solution)/shard_map/along_width/pallas_call | solution.py:159
  17.7 0.0 copy-start.1
  17.7 11.3 %all-to-all-start = ((f32[32,2,64,128]{3,2,1,0:T(8,128)}), f32[32,2,64,128]{3,2,1,0:T(8,128)S(1)}, u32[]{:S(2)}, u32[]{:S(2)}) async-start(f32[32,2,64,128]{3,2,1,0:T(8,128)} %get-tuple-element.7), calls=%async_computation | async-start | bytes 4194304 | tf_op jit(solution)/shard_map/all_to_all | solution.py:336
  29.7 0.0 copy-done.1
  29.8 0.1 convert_element_type.40
  29.8 0.1 copy.25
  29.9 0.1 slice_reduce_fusion
  30.0 0.1 reshape_squeeze.4
  30.1 0.2 convert_reduce_fusion
  30.3 8.7 %multiply_multiply_fusion = (f32[32,1,128,128]{3,2,1,0:T(8,128)S(1)}, f32[32,1,128,128]{3,2,1,0:T(8,128)S(1)}) fusion(f32[128]{0:T(128)S(1)} %convert_reduce_fusion, f32[32,128]{1,0:T(8,128)S(1)} %copy.25, s32[128]{0:T(128)S(1)} %fusion.3, s32[32,128]{1,0:T(8,128)S(1)} %fusion.2, f32[]{:T(128)} %bitcast), kind=kLoop, calls=%fused_computation.3 | loop fusion | flops 7340032 | bytes 4228100 | tf_op jit(solution)/shard_map/mul | solution.py:328
  39.0 2.4 %pad_maximum_fusion = (f32[32,2,64,128]{3,2,1,0:T(8,128)}, f32[32,2,64,128]{3,2,1,0:T(8,128)}) fusion(f32[32,1,128,128]{3,2,1,0:T(8,128)S(1)} %get-tuple-element.11, f32[32,1,128,128]{3,2,1,0:T(8,128)S(1)} %get-tuple-element.12), kind=kLoop, calls=%fused_computation.7 | loop fusion | flops 1048576 | bytes 8388608 | tf_op jit(solution)/shard_map/stack | solution.py:328
  41.4 39.4 %all-to-all-done.x_ref = f32[32,2,64,128]{3,2,1,0:T(8,128)S(1)} async-done(((f32[32,2,64,128]{3,2,1,0:T(8,128)}), f32[32,2,64,128]{3,2,1,0:T(8,128)S(1)}, u32[]{:S(2)}, u32[]{:S(2)}) %all-to-all-start) | async-done | bytes 2097184 | tf_op jit(solution)/shard_map/all_to_all | solution.py:336
  80.9 0.0 copy-start
  80.9 1.3 copy-done
  82.2 5.4 %all-to-all-start.1 = ((f32[32,2,64,128]{3,2,1,0:T(8,128)}), f32[32,2,64,128]{3,2,1,0:T(8,128)}, u32[]{:S(2)}, u32[]{:S(2)}) async-start(f32[32,2,64,128]{3,2,1,0:T(8,128)} %get-tuple-element.8), calls=%async_computation.2 | async-start | bytes 4194304 | tf_op jit(solution)/shard_map/all_to_all | solution.py:336
  87.5 0.2 reduce-scatter.3.cloned.1.call-start
  87.8 6.8 %along_height.2 = f32[32,2,64,128]{3,2,1,0:T(8,128)} custom-call(f32[32,2,64,128]{3,2,1,0:T(8,128)} %copy-done, f32[32,2,64,128]{3,2,1,0:T(8,128)} %get-tuple-element.10.h_ref, f32[2,32,128]{2,1,0:T(8,128)} %constant.48.clone.tw_ref.ftw_ref, bf16[256,256]{1,0:T(8,128)(2,1)} %constant.49.clone.high_ref.fh_ref, ...), custom_call_target="tpu_custom_call" | custom-call | flops 3221225472 | bytes 6291456 | tf_op jit(solution)/shard_map/along_height/pallas_call | solution.py:236
  94.5 0.0 reduce-scatter.3.cloned.1.call-update
  94.6 0.0 reduce-scatter.5.cloned.1.call-start
  94.6 44.3 %all-to-all-done.1.x_ref = f32[32,2,64,128]{3,2,1,0:T(8,128)} async-done(((f32[32,2,64,128]{3,2,1,0:T(8,128)}), f32[32,2,64,128]{3,2,1,0:T(8,128)}, u32[]{:S(2)}, u32[]{:S(2)}) %all-to-all-start.1) | async-done | bytes 2097184 | tf_op jit(solution)/shard_map/all_to_all | solution.py:336
  138.9 6.7 %along_height.3 = f32[32,2,64,128]{3,2,1,0:T(8,128)} custom-call(f32[32,2,64,128]{3,2,1,0:T(8,128)} %all-to-all-done.1.x_ref, f32[32,2,64,128]{3,2,1,0:T(8,128)} %get-tuple-element.9.h_ref, f32[2,32,128]{2,1,0:T(8,128)} %constant.48.clone.tw_ref.ftw_ref, bf16[256,256]{1,0:T(8,128)(2,1)} %constant.49.clone.high_ref.fh_ref, ...), custom_call_target="tpu_custom_call" | custom-call | flops 3221225472 | bytes 6291456 | tf_op jit(solution)/shard_map/along_height/pallas_call | solution.py:236
  145.6 0.0 reduce-scatter.5.cloned.1.call-update
  145.6 0.0 reduce-scatter.3.cloned.1.call-done.refs_0_
  145.7 42.0 %reduce-scatter.5.cloned.1.call-done.refs_1_ = f32[4,2,64,128]{3,2,1,0:T(8,128)} async-done(((f32[32,2,64,128]{3,2,1,0:T(8,128)}), f32[4,2,64,128]{3,2,1,0:T(8,128)}) %reduce-scatter.5.cloned.1.call-update) | async-done | bytes 262160 | tf_op jit(solution)/shard_map/reduce_scatter | solution.py:338
  187.7 2.0 flip.1
  189.7 32.4 %all_to_all.15.x_ref = f32[64,2,8,128]{3,2,1,0:T(8,128)} all-to-all(f32[64,2,8,128]{3,2,1,0:T(8,128)} %flip.1), channel_id=1, replica_groups=mesh['depth_0'=8,'depth_1'=2,'rows'=32] {'depth_1','rows'}, dimensions={0} | all-to-all | bytes 1048576 | tf_op jit(solution)/shard_map/all_to_all | solution.py:339
  222.2 2.2 inverse_width.1
  (4 shorter events, 0.1 us)
Async XLA Ops:
  17.7 12.0 %copy-start.1 = (s32[1,2,4096]{2,1,0:T(2,128)S(1)}, s32[1,2,4096]{2,1,0:T(2,128)}, u32[]{:S(2)}) copy-start(s32[1,2,4096]{2,1,0:T(2,128)} %param.23) | copy-start | bytes 98308
  17.7 63.1 %all-to-all-start = ((f32[32,2,64,128]{3,2,1,0:T(8,128)}), f32[32,2,64,128]{3,2,1,0:T(8,128)S(1)}, u32[]{:S(2)}, u32[]{:S(2)}) async-start(f32[32,2,64,128]{3,2,1,0:T(8,128)} %get-tuple-element.7), calls=%async_computation | async-start | bytes 4194304 | tf_op jit(solution)/shard_map/all_to_all | solution.py:336
  80.9 1.3 copy-start
  82.2 56.7 %all-to-all-start.1 = ((f32[32,2,64,128]{3,2,1,0:T(8,128)}), f32[32,2,64,128]{3,2,1,0:T(8,128)}, u32[]{:S(2)}, u32[]{:S(2)}) async-start(f32[32,2,64,128]{3,2,1,0:T(8,128)} %get-tuple-element.8), calls=%async_computation.2 | async-start | bytes 4194304 | tf_op jit(solution)/shard_map/all_to_all | solution.py:336
  87.5 58.1 %reduce-scatter.3.cloned.1.call-start = ((), (), s32[]{:S(2)}) async-start(), calls=%async_computation.5 | async-start | bytes 2359296 | tf_op jit(solution)/shard_map/reduce_scatter | solution.py:338
  94.6 93.1 %reduce-scatter.5.cloned.1.call-start = ((), (), s32[]{:S(2)}) async-start(), calls=%async_computation.6 | async-start | bytes 2359296 | tf_op jit(solution)/shard_map/reduce_scatter | solution.py:338
Sparse Core Ops, SparseCore 0:
  94.7 46.0 reduce-scatter.2
  145.8 41.8 reduce-scatter.4
where the time goes:
time: 232 us; the launch traced here: 231 us
  waiting for transfers between devices  126 us (54%)
  blocking collectives  32.4 us (14%)
  Pallas kernels  28.8 us (12%)
  starting transfers between devices  17 us (7%)
  between operations  14.1 us (6%)
  other arithmetic  11.4 us (5%)
    all_to_all x2, waiting for transfers between devices, local(): lax.all_to_all(spectra[i], 'rows', split_axis=0, concat_axis=0, tiled=True)  83.7 us
    reduce_scatter x2, waiting for transfers between devices, local(): lax.psum_scatter(part, 'depth_0', scatter_dimension=0, tiled=True)  42.1 us
    all_to_all x1, blocking collectives, local(): lax.all_to_all(flip(shares), ('depth_1', 'rows'), split_axis=0, concat_ax...  32.4 us
    all_to_all x2, starting transfers between devices, local(): lax.all_to_all(spectra[i], 'rows', split_axis=0, concat_axis=0, tiled=True)  16.7 us
    pallas_call x2, Pallas kernels, along_height(): pl.pallas_call(height_kernel, name='along_height', grid=(count // HEIGHT_...  13.5 us
    pallas_call x1, Pallas kernels, along_width(): pl.pallas_call(width_kernel, name='along_width', grid=(2 * WIDTH_STEPS,),...  11.2 us
    mul x1, other arithmetic, transfer_factors(): jnp.sin(angles) * weights  8.73 us
  transfers between devices with their start and end apart: 4, of which 3 were waited for; matrix products, arithmetic and copies ran while one was open for 5% of the time, Pallas kernels for 6%

commit v1 on v0

--- a/solution.py
+++ b/solution.py
@@ -15,8 +15,8 @@
 N = 4096
 DEPTH = ("depth_0", "depth_1")
 DEPTH_ROWS = ("depth_0", "depth_1", "rows")
-CHUNKS = 2
-KC = HIGH // CHUNKS
+CHUNKS = (96, 32)
+STARTS = (0, 96)
 
 
 def block_table(direction, scaling):
@@ -113,7 +113,7 @@
 
 
 def width_kernel(x_ref, tw_ref, high_ref, low_ref, *rest):
-    out_refs, (mid_ref, part_ref) = rest[:CHUNKS], rest[CHUNKS:]
+    out_refs, (mid_ref, part_ref) = rest[: len(CHUNKS)], rest[len(CHUNKS) :]
     step = pl.program_id(0)
 
     @pl.when(step < WIDTH_STEPS)
@@ -142,8 +142,8 @@
             done = product(mid_ref[base + k], (high_ref, low_ref))
             for c in range(2):
                 flat = done[:, HIGH * c : HIGH * (c + 1)].T
-                for i in range(CHUNKS):
-                    out_refs[i][k, c] = flat[KC * i : KC * (i + 1)]
+                for out_ref, start, count in zip(out_refs, STARTS, CHUNKS):
+                    out_ref[k, c] = flat[start : start + count]
 
 
 def whole(*dims):
@@ -152,10 +152,13 @@
 
 def along_width(target):
     high, low = block_table(-1.0, 1.0 / 64)
-    shape = jax.ShapeDtypeStruct((LOW, 2, KC, HIGH), jnp.float32)
-    spec = pl.BlockSpec(
-        (WIDTH_LOWS, 2, KC, HIGH), lambda i: (jnp.maximum(i - WIDTH_STEPS, 0), 0, 0, 0)
-    )
+    shapes = [jax.ShapeDtypeStruct((LOW, 2, count, HIGH), jnp.float32) for count in CHUNKS]
+    specs = [
+        pl.BlockSpec(
+            (WIDTH_LOWS, 2, count, HIGH), lambda i: (jnp.maximum(i - WIDTH_STEPS, 0), 0, 0, 0)
+        )
+        for count in CHUNKS
+    ]
     return pl.pallas_call(
         width_kernel,
         name="along_width",
@@ -168,8 +171,8 @@
             whole(2 * HIGH, 2 * HIGH),
             whole(2 * HIGH, 2 * HIGH),
         ],
-        out_specs=[spec] * CHUNKS,
-        out_shape=[shape] * CHUNKS,
+        out_specs=specs,
+        out_shape=shapes,
         scratch_shapes=[
             pltpu.VMEM((LOW, HIGH, 2 * HIGH), jnp.float32),
             pltpu.VMEM((WIDTH_ROWS // 8, LOW, 2, 8, HIGH), jnp.float32),
@@ -259,21 +262,22 @@
     )
 
 
-def flip_kernel(*refs):
-    in_refs, out_ref = refs[:-1], refs[-1]
-    for n in range(out_ref.shape[0] // 16):
+def flip_kernel(share_ref, parts_ref, out_ref):
+    for n in range(4):
         for c in range(2):
-            whole_tile = jnp.concatenate([ref[n, c] for ref in in_refs], axis=0)
-            out_ref[16 * n : 16 * n + 16, c] = whole_tile.T.reshape(16, 8, HIGH)
-
-
-def flip(shares):
-    count = 16 * shares[0].shape[0]
+            total = parts_ref[n, c]
+            for source in range(1, 8):
+                total = total + parts_ref[4 * source + n, c]
+            tile = jnp.concatenate([share_ref[n, c], total], axis=0)
+            out_ref[16 * n : 16 * n + 16, c] = tile.T.reshape(16, 8, HIGH)
+
+
+def flip(share, parts):
     return pl.pallas_call(
         flip_kernel,
         name="flip",
-        out_shape=jax.ShapeDtypeStruct((count, 2, 8, HIGH), jnp.float32),
-    )(*shares)
+        out_shape=jax.ShapeDtypeStruct((64, 2, 8, HIGH), jnp.float32),
+    )(share, parts)
 
 
 def inverse_width_kernel(x_ref, tw_ref, high_ref, low_ref, out_ref, mid_ref, part_ref):
@@ -310,11 +314,11 @@
     return jnp.where(natural < N // 2, natural, natural - N)
 
 
-def transfer_factors(depth_index, band_mask, column):
+def transfer_factors(depth_index, band_mask, column, start, count):
     high = jnp.arange(HIGH, dtype=jnp.int32)
     low = jnp.arange(LOW, dtype=jnp.int32)
     height = signed(low[:, None] + LOW * high[None, :])
-    width = signed(column + LOW * high)
+    width = signed(column + LOW * (start + jnp.arange(count, dtype=jnp.int32)))
     square = (height * height)[:, None, :] + (width * width)[None, :, None]
     square = square.astype(jnp.float32) * np.float32(1.0 / (N * N))
     descent = -square / (jnp.sqrt(4.0 - square) + 2.0)
@@ -323,21 +327,25 @@
     mask_height = band_mask[0, 0].reshape(HIGH, LOW).T.astype(jnp.float32)
     mask_width = lax.dynamic_slice_in_dim(
         band_mask[0, 1].reshape(HIGH, LOW).T, column, 1, 0
-    )[0].astype(jnp.float32)
+    )[0, start : start + count].astype(jnp.float32)
     weights = mask_height[:, None, :] * mask_width[None, :, None]
     return jnp.stack([jnp.cos(angles) * weights, jnp.sin(angles) * weights], axis=1)
 
 
-def local(target, depth_index, band_mask):
+def hologram(target, depth_index, band_mask):
     spectra = along_width(target)
-    transfer = transfer_factors(depth_index, band_mask, lax.axis_index("rows"))
-    shares = []
-    for i in range(CHUNKS):
-        columns = lax.all_to_all(spectra[i], "rows", split_axis=0, concat_axis=0, tiled=True)
-        part = along_height(columns, transfer[:, :, KC * i : KC * (i + 1)])
-        shares.append(lax.psum_scatter(part, "depth_0", scatter_dimension=0, tiled=True))
+    transfer = [
+        transfer_factors(depth_index, band_mask, lax.axis_index("rows"), start, count)
+        for start, count in zip(STARTS, CHUNKS)
+    ]
+    parts = []
+    for i, (block, start, count) in enumerate(zip(spectra, STARTS, CHUNKS)):
+        columns = lax.all_to_all(block, "rows", split_axis=0, concat_axis=0, tiled=True)
+        parts.append(along_height(columns, transfer[i]))
+    share = lax.psum_scatter(parts[0], "depth_0", scatter_dimension=0, tiled=True)
+    rest = lax.all_to_all(parts[1], "depth_0", split_axis=0, concat_axis=0, tiled=True)
     pieces = lax.all_to_all(
-        flip(shares), ("depth_1", "rows"), split_axis=0, concat_axis=0, tiled=True
+        flip(share, rest), ("depth_1", "rows"), split_axis=0, concat_axis=0, tiled=True
     )
     return inverse_width(pieces, 1.0 / math.sqrt(lax.axis_size(DEPTH)))
 
@@ -346,4 +354,4 @@
     split = Mesh(mesh.devices.reshape(8, 2, mesh.shape["rows"]), ("depth_0", "depth_1", "rows"))
     in_specs = (P(DEPTH, None, "rows", None), P(DEPTH), P(DEPTH, None, None))
     out_specs = P(None, DEPTH_ROWS, None)
-    return jax.shard_map(local, mesh=split, in_specs=in_specs, out_specs=out_specs, check_vma=False)
+    return jax.shard_map(hologram, mesh=split, in_specs=in_specs, out_specs=out_specs, check_vma=False)

time: 232 us -> 229 us (0.987)
  waiting for transfers between devices: 126 us -> 90 us
  blocking collectives: 32.4 us -> 63.1 us
    reduce_scatter x2 -> x1, waiting for transfers between devices: 42.1 us -> 0.01 us  [hologram(): lax.psum_scatter(parts[0], 'depth_0', scatter_dimension=0, tiled=True)]
    all_to_all x1 -> x2, blocking collectives: 32.4 us -> 63.1 us  [the longest x1 36.6 us: hologram(): lax.all_to_all(parts[1], 'depth_0', split_axis=0, concat_axis=0, tiled=True)]
    all_to_all x2, waiting for transfers between devices: 83.7 us -> 90 us  [hologram(): lax.all_to_all(block, 'rows', split_axis=0, concat_axis=0, tiled=True)]
    mul x1 -> x2, other arithmetic: 8.73 us -> 8.82 us  [transfer_factors(): jnp.cos(angles) * weights]
  transfers between devices with their start and end apart: 4 -> 3, of which waited for: 3 -> 2; matrix products, arithmetic and copies ran while one was open for 5% -> 5% of each run, Pallas kernels for 6% -> 2%
where the time goes in v1:
time: 229 us; the launch traced here: 228 us
  waiting for transfers between devices  90 us (39%)
  blocking collectives  63.1 us (28%)
  Pallas kernels  29.1 us (13%)
  starting transfers between devices  16.8 us (7%)
  between operations  14.2 us (6%)
  other arithmetic  11.9 us (5%)
  local copies, waits for them, and re-layouts  3.13 us (1%)
    all_to_all x2, waiting for transfers between devices, hologram(): lax.all_to_all(block, 'rows', split_axis=0, concat_axis=0, tiled=True)  90 us
    all_to_all x1, blocking collectives, hologram(): lax.all_to_all(parts[1], 'depth_0', split_axis=0, concat_axis=0, tiled=True)  36.6 us
    all_to_all x1, blocking collectives, hologram(): lax.all_to_all(flip(share, rest), ('depth_1', 'rows'), split_axis=0, conc...  26.5 us
    all_to_all x2, starting transfers between devices, hologram(): lax.all_to_all(block, 'rows', split_axis=0, concat_axis=0, tiled=True)  16.8 us
    pallas_call x2, Pallas kernels, along_height(): pl.pallas_call(height_kernel, name='along_height', grid=(count // HEIGHT_...  13.4 us
    pallas_call x1, Pallas kernels, along_width(): pl.pallas_call(width_kernel, name='along_width', grid=(2 * WIDTH_STEPS,),...  11.2 us
    mul x2, other arithmetic, transfer_factors(): jnp.cos(angles) * weights  8.82 us
  transfers between devices with their start and end apart: 3, of which 2 were waited for; matrix products, arithmetic and copies ran while one was open for 5% of the time, Pallas kernels for 2%

profile of v1, /device:TPU:1, one launch (start us, length us, event | category | flops | bytes accessed | tf_op | source)
XLA Modules:
  0.0 228.3 jit_solution(2785131667225063401)
XLA Ops:
  6.5 11.2 %along_width.1 = (f32[32,2,96,128]{3,2,1,0:T(8,128)}, f32[32,2,32,128]{3,2,1,0:T(8,128)}) custom-call(f32[1,2,128,4096]{3,2,1,0:T(8,128)} %x_ref.1, f32[2,32,128]{2,1,0:T(8,128)} %constant.14.clone.tw_ref.ftw_ref, bf16[256,256]{1,0:T(8,128)(2,1)} %constant.15.clone.high_ref.fh_ref, bf16[256,256]{1,0:T(8,128)(2,1)} %constant.16.clone.low_ref.fl_ref), custom_call_target="tpu_custom_call" | custom-call | flops 3221225472 | bytes 8388608 | tf_op jit(solution)/shard_map/along_width/pallas_call | solution.py:162
  17.7 0.0 copy-start.2
  17.7 11.3 %all-to-all-start = ((f32[32,2,96,128]{3,2,1,0:T(8,128)}), f32[32,2,96,128]{3,2,1,0:T(8,128)S(1)}, u32[]{:S(2)}, u32[]{:S(2)}) async-start(f32[32,2,96,128]{3,2,1,0:T(8,128)} %get-tuple-element.7), calls=%async_computation | async-start | bytes 6291456 | tf_op jit(solution)/shard_map/all_to_all | solution.py:343
  29.1 0.0 reduce-scatter.2.cloned.1.call-start
  29.1 0.0 copy-done.2
  29.2 0.1 reshape_squeeze.2
  29.3 0.1 convert_element_type.66
  29.4 0.1 copy.26
  30.2 0.2 dynamic-slice_reduce_fusion
  30.4 6.6 %multiply_multiply_fusion.1 = (f32[32,1,96,128]{3,2,1,0:T(8,128)S(1)}, f32[32,1,96,128]{3,2,1,0:T(8,128)S(1)}) fusion(f32[96]{0:T(128)S(1)} %convert_bitcast_fusion.1, f32[32,128]{1,0:T(8,128)S(1)} %copy.26, s32[96]{0:T(128)S(1)} %fusion.3, s32[32,128]{1,0:T(8,128)S(1)} %fusion.2, f32[]{:T(128)} %bitcast), kind=kLoop, calls=%fused_computation.3 | loop fusion | flops 5505024 | bytes 3179268 | tf_op jit(solution)/shard_map/mul | solution.py:332
  37.0 1.9 pad_maximum_fusion.h_ref
  38.8 64.5 %all-to-all-done.x_ref = f32[32,2,96,128]{3,2,1,0:T(8,128)S(1)} async-done(((f32[32,2,96,128]{3,2,1,0:T(8,128)}), f32[32,2,96,128]{3,2,1,0:T(8,128)S(1)}, u32[]{:S(2)}, u32[]{:S(2)}) %all-to-all-start) | async-done | bytes 3145760 | tf_op jit(solution)/shard_map/all_to_all | solution.py:343
  103.4 0.0 copy-start
  103.4 1.7 copy-done
  105.1 9.2 %along_height.2 = f32[32,2,96,128]{3,2,1,0:T(8,128)} custom-call(f32[32,2,96,128]{3,2,1,0:T(8,128)} %copy-done, f32[32,2,96,128]{3,2,1,0:T(8,128)} %pad_maximum_fusion.h_ref, f32[2,32,128]{2,1,0:T(8,128)} %constant.14.clone.tw_ref.ftw_ref, bf16[256,256]{1,0:T(8,128)(2,1)} %constant.15.clone.high_ref.fh_ref, bf16[256,256]{1,0:T(8,128)(2,1)} %constant.16.clone.low_ref.fl_ref, ...), custom_call_target="tpu_custom_call" | custom-call | flops 4831838208 | bytes 9437184 | tf_op jit(solution)/shard_map/along_height/pallas_call | solution.py:239
  114.3 0.0 reduce-scatter.2.cloned.1.call-update
  114.3 5.5 %all-to-all-start.1 = ((f32[32,2,32,128]{3,2,1,0:T(8,128)}), f32[32,2,32,128]{3,2,1,0:T(8,128)S(1)}, u32[]{:S(2)}, u32[]{:S(2)}) async-start(f32[32,2,32,128]{3,2,1,0:T(8,128)} %get-tuple-element.8), calls=%async_computation.2 | async-start | bytes 2097152 | tf_op jit(solution)/shard_map/all_to_all | solution.py:343
  119.8 0.1 convert_bitcast_fusion
  119.8 2.3 multiply_multiply_fusion.3
  122.1 1.1 pad_maximum_fusion.1.h_ref
  123.2 25.4 %all-to-all-done.1.x_ref = f32[32,2,32,128]{3,2,1,0:T(8,128)S(1)} async-done(((f32[32,2,32,128]{3,2,1,0:T(8,128)}), f32[32,2,32,128]{3,2,1,0:T(8,128)S(1)}, u32[]{:S(2)}, u32[]{:S(2)}) %all-to-all-start.1) | async-done | bytes 1048608 | tf_op jit(solution)/shard_map/all_to_all | solution.py:343
  148.6 0.0 copy-start.1
  148.6 1.0 copy-done.1
  149.6 4.2 %along_height.3 = f32[32,2,32,128]{3,2,1,0:T(8,128)} custom-call(f32[32,2,32,128]{3,2,1,0:T(8,128)} %copy-done.1, f32[32,2,32,128]{3,2,1,0:T(8,128)} %pad_maximum_fusion.1.h_ref, f32[2,32,128]{2,1,0:T(8,128)} %constant.14.clone.tw_ref.ftw_ref, bf16[256,256]{1,0:T(8,128)(2,1)} %constant.15.clone.high_ref.fh_ref, ...), custom_call_target="tpu_custom_call" | custom-call | flops 1610612736 | bytes 3145728 | tf_op jit(solution)/shard_map/along_height/pallas_call | solution.py:239
  153.8 36.6 %all_to_all.20.parts_ref = f32[32,2,32,128]{3,2,1,0:T(8,128)} all-to-all(f32[32,2,32,128]{3,2,1,0:T(8,128)} %along_height.3), channel_id=1, replica_groups=mesh['depth_0'=8,'depth_1'=2,'rows'=32] {'depth_0'}, dimensions={0} | all-to-all | bytes 2097152 | tf_op jit(solution)/shard_map/all_to_all | solution.py:346
  190.5 0.0 reduce-scatter.2.cloned.1.call-done.share_ref
  190.5 2.3 %flip.1 = f32[64,2,8,128]{3,2,1,0:T(8,128)} custom-call(f32[4,2,96,128]{3,2,1,0:T(8,128)} %reduce-scatter.2.cloned.1.call-done.share_ref, f32[32,2,32,128]{3,2,1,0:T(8,128)} %all_to_all.20.parts_ref), custom_call_target="tpu_custom_call" | custom-call | tf_op jit(solution)/shard_map/flip/pallas_call | solution.py:276
  192.8 26.5 %all_to_all.21.x_ref = f32[64,2,8,128]{3,2,1,0:T(8,128)} all-to-all(f32[64,2,8,128]{3,2,1,0:T(8,128)} %flip.1), channel_id=1, replica_groups=mesh['depth_0'=8,'depth_1'=2,'rows'=32] {'depth_1','rows'}, dimensions={0} | all-to-all | bytes 1048576 | tf_op jit(solution)/shard_map/all_to_all | solution.py:347
  219.3 2.2 inverse_width.1
  (7 shorter events, 0.1 us)
Async XLA Ops:
  17.7 11.4 %copy-start.2 = (s32[1,2,4096]{2,1,0:T(2,128)S(1)}, s32[1,2,4096]{2,1,0:T(2,128)}, u32[]{:S(2)}) copy-start(s32[1,2,4096]{2,1,0:T(2,128)} %param.23) | copy-start | bytes 98308
  17.7 85.6 %all-to-all-start = ((f32[32,2,96,128]{3,2,1,0:T(8,128)}), f32[32,2,96,128]{3,2,1,0:T(8,128)S(1)}, u32[]{:S(2)}, u32[]{:S(2)}) async-start(f32[32,2,96,128]{3,2,1,0:T(8,128)} %get-tuple-element.7), calls=%async_computation | async-start | bytes 6291456 | tf_op jit(solution)/shard_map/all_to_all | solution.py:343
  29.1 161.4 %reduce-scatter.2.cloned.1.call-start = ((), (), s32[]{:S(2)}) async-start(), calls=%async_computation.5 | async-start | bytes 3538944 | tf_op jit(solution)/shard_map/reduce_scatter | solution.py:345
  103.4 1.7 copy-start
  114.3 34.3 %all-to-all-start.1 = ((f32[32,2,32,128]{3,2,1,0:T(8,128)}), f32[32,2,32,128]{3,2,1,0:T(8,128)S(1)}, u32[]{:S(2)}, u32[]{:S(2)}) async-start(f32[32,2,32,128]{3,2,1,0:T(8,128)} %get-tuple-element.8), calls=%async_computation.2 | async-start | bytes 2097152 | tf_op jit(solution)/shard_map/all_to_all | solution.py:343
  148.6 1.0 copy-start.1
Sparse Core Ops, SparseCore 0:
  114.4 47.2 reduce-scatter.1

commit v2 on v1

--- a/solution.py
+++ b/solution.py
@@ -15,8 +15,9 @@
 N = 4096
 DEPTH = ("depth_0", "depth_1")
 DEPTH_ROWS = ("depth_0", "depth_1", "rows")
-CHUNKS = (96, 32)
-STARTS = (0, 96)
+CHUNKS = (64, 64)
+STARTS = (0, 64)
+PARTS = ((64,), (32, 32))
 
 
 def block_table(direction, scaling):
@@ -107,7 +108,7 @@
     return dot(high, high_table) + (dot(low, high_table) + dot(high, low_table))
 
 
-WIDTH_ROWS = 16
+WIDTH_ROWS = 32
 WIDTH_STEPS = HIGH // WIDTH_ROWS
 WIDTH_LOWS = LOW // WIDTH_STEPS
 
@@ -231,16 +232,18 @@
         low_transform(load, store, part_ref.at[g], 1)
 
 
-def along_height(columns, transfer):
-    spec = pl.BlockSpec((LOW, 2, HEIGHT_ROWS, HIGH), lambda i: (0, 0, i, 0))
+def along_height(columns, transfer, start, count):
+    first = start // HEIGHT_ROWS
+    block = (LOW, 2, HEIGHT_ROWS, HIGH)
+    spec = pl.BlockSpec(block, lambda i: (0, 0, i, 0))
+    moved = pl.BlockSpec(block, lambda i: (0, 0, i + first, 0))
     table = whole(2 * HIGH, 2 * HIGH)
     forward, backward = block_table(-1.0, 1.0 / 64), block_table(1.0, 1.0 / 64)
-    count = columns.shape[2]
     return pl.pallas_call(
         height_kernel,
         name="along_height",
         grid=(count // HEIGHT_ROWS,),
-        in_specs=[spec, spec, whole(2, LOW, HIGH), table, table, whole(2, LOW, HIGH), table, table],
+        in_specs=[moved, moved, whole(2, LOW, HIGH), table, table, whole(2, LOW, HIGH), table, table],
         out_specs=spec,
         out_shape=jax.ShapeDtypeStruct((LOW, 2, count, HIGH), jnp.float32),
         scratch_shapes=[
@@ -262,22 +265,30 @@
     )
 
 
-def flip_kernel(share_ref, parts_ref, out_ref):
-    for n in range(4):
-        for c in range(2):
-            total = parts_ref[n, c]
-            for source in range(1, 8):
-                total = total + parts_ref[4 * source + n, c]
-            tile = jnp.concatenate([share_ref[n, c], total], axis=0)
-            out_ref[16 * n : 16 * n + 16, c] = tile.T.reshape(16, 8, HIGH)
-
-
-def flip(share, parts):
+def flip_kernel(*refs):
+    in_refs, out_ref = refs[:-1], refs[-1]
+    for c in range(2):
+        tiles = []
+        for ref in in_refs:
+            total = ref[0, 0, c]
+            for source in range(1, ref.shape[0]):
+                total = total + ref[source, 0, c]
+            tiles.append(total)
+        out_ref[:, c] = jnp.concatenate(tiles, axis=0).T.reshape(16, 8, HIGH)
+
+
+def flip(parts):
     return pl.pallas_call(
         flip_kernel,
         name="flip",
+        grid=(4,),
+        in_specs=[
+            pl.BlockSpec((part.shape[0], 1) + part.shape[2:], lambda i: (0, i, 0, 0, 0))
+            for part in parts
+        ],
+        out_specs=pl.BlockSpec((16, 2, 8, HIGH), lambda i: (i, 0, 0, 0)),
         out_shape=jax.ShapeDtypeStruct((64, 2, 8, HIGH), jnp.float32),
-    )(share, parts)
+    )(*parts)
 
 
 def inverse_width_kernel(x_ref, tw_ref, high_ref, low_ref, out_ref, mid_ref, part_ref):
@@ -334,18 +345,25 @@
 
 def hologram(target, depth_index, band_mask):
     spectra = along_width(target)
-    transfer = [
-        transfer_factors(depth_index, band_mask, lax.axis_index("rows"), start, count)
-        for start, count in zip(STARTS, CHUNKS)
-    ]
-    parts = []
-    for i, (block, start, count) in enumerate(zip(spectra, STARTS, CHUNKS)):
+    transfer = []
+    for start, count in zip(STARTS, CHUNKS):
+        column = lax.axis_index("rows")
+        transfer.append(transfer_factors(depth_index, band_mask, column, start, count))
+    shares = []
+    for i, block in enumerate(spectra):
         columns = lax.all_to_all(block, "rows", split_axis=0, concat_axis=0, tiled=True)
-        parts.append(along_height(columns, transfer[i]))
-    share = lax.psum_scatter(parts[0], "depth_0", scatter_dimension=0, tiled=True)
-    rest = lax.all_to_all(parts[1], "depth_0", split_axis=0, concat_axis=0, tiled=True)
+        start = 0
+        for j, count in enumerate(PARTS[i]):
+            part = along_height(columns, transfer[i], start, count)
+            start += count
+            if j == 0:
+                share = lax.psum_scatter(part, "depth_0", scatter_dimension=0, tiled=True)
+                shares.append(share[None])
+            else:
+                share = lax.all_to_all(part, "depth_0", split_axis=0, concat_axis=0, tiled=True)
+                shares.append(share.reshape(8, 4, 2, count, HIGH))
     pieces = lax.all_to_all(
-        flip(share, rest), ("depth_1", "rows"), split_axis=0, concat_axis=0, tiled=True
+        flip(shares), ("depth_1", "rows"), split_axis=0, concat_axis=0, tiled=True
     )
     return inverse_width(pieces, 1.0 / math.sqrt(lax.axis_size(DEPTH)))
 

time: 229 us -> 244 us (1.066)
  blocking collectives: 63.1 us -> 135 us
  waiting for transfers between devices: 90 us -> 46.3 us
  starting transfers between devices: 16.8 us -> 6.26 us
  local copies, waits for them, and re-layouts: 3.13 us -> 0.44 us
    all_to_all x2 -> x3, blocking collectives: 63.1 us -> 135 us  [the longest x1 62.6 us: hologram(): lax.all_to_all(block, 'rows', split_axis=0, concat_axis=0, tiled=True)]
    all_to_all x2 -> x1, waiting for transfers between devices: 90 us -> 34.3 us  [hologram(): lax.all_to_all(block, 'rows', split_axis=0, concat_axis=0, tiled=True)]
    reduce_scatter x1 -> x2, waiting for transfers between devices: 0.01 us -> 12 us  [hologram(): share = lax.psum_scatter(part, 'depth_0', scatter_dimension=0, tiled=True)]
    all_to_all x2 -> x1, starting transfers between devices: 16.8 us -> 6 us  [hologram(): lax.all_to_all(block, 'rows', split_axis=0, concat_axis=0, tiled=True)]
    pallas_call x1, Pallas kernels: 11.2 us -> 7.98 us  [along_width(): pl.pallas_call(width_kernel, name='along_width', grid=(2 * WIDTH_STEPS,),...]
    unnamed x6 -> x2, local copies, waits for them, and re-layouts: 2.7 us -> 0.01 us
    pallas_call x2 -> x3, Pallas kernels: 13.4 us -> 15.1 us  [along_height(): pl.pallas_call(height_kernel, name='along_height', grid=(count // HEIGHT_...]
    mul x2 -> x1, other arithmetic: 8.82 us -> 8.73 us  [transfer_factors(): jnp.cos(angles) * weights]
  transfers between devices with their start and end apart: 3 -> 3, of which waited for: 2 -> 2; matrix products, arithmetic and copies ran while one was open for 5% -> 5% of each run, Pallas kernels for 2% -> 6%
where the time goes in v2:
time: 244 us; the launch traced here: 243 us
  blocking collectives  135 us (55%)
  waiting for transfers between devices  46.3 us (19%)
  Pallas kernels  28.8 us (12%)
  between operations  14.2 us (6%)
  other arithmetic  11.8 us (5%)
  starting transfers between devices  6.26 us (3%)
    all_to_all x1, blocking collectives, hologram(): lax.all_to_all(block, 'rows', split_axis=0, concat_axis=0, tiled=True)  62.6 us
    all_to_all x1, blocking collectives, hologram(): lax.all_to_all(part, 'depth_0', split_axis=0, concat_axis=0, tiled=True)  46.5 us
    all_to_all x1, waiting for transfers between devices, hologram(): lax.all_to_all(block, 'rows', split_axis=0, concat_axis=0, tiled=True)  34.3 us
    all_to_all x1, blocking collectives, hologram(): lax.all_to_all(flip(shares), ('depth_1', 'rows'), split_axis=0, concat_ax...  26.4 us
    pallas_call x3, Pallas kernels, along_height(): pl.pallas_call(height_kernel, name='along_height', grid=(count // HEIGHT_...  15.1 us
    reduce_scatter x2, waiting for transfers between devices, hologram(): share = lax.psum_scatter(part, 'depth_0', scatter_dimension=0, tiled=True)  12 us
    mul x1, other arithmetic, transfer_factors(): jnp.cos(angles) * weights  8.73 us
    pallas_call x1, Pallas kernels, along_width(): pl.pallas_call(width_kernel, name='along_width', grid=(2 * WIDTH_STEPS,),...  7.98 us
  transfers between devices with their start and end apart: 3, of which 2 were waited for; matrix products, arithmetic and copies ran while one was open for 5% of the time, Pallas kernels for 6%

profile of v2, /device:TPU:1, one launch (start us, length us, event | category | flops | bytes accessed | tf_op | source)
XLA Modules:
  0.0 243.3 jit_solution(5560091601816449358)
XLA Ops:
  6.5 8.0 %along_width.1 = (f32[32,2,64,128]{3,2,1,0:T(8,128)}, f32[32,2,64,128]{3,2,1,0:T(8,128)}) custom-call(f32[1,2,128,4096]{3,2,1,0:T(8,128)} %x_ref.1, f32[2,32,128]{2,1,0:T(8,128)} %constant.51.clone.tw_ref.ftw_ref, bf16[256,256]{1,0:T(8,128)(2,1)} %constant.52.clone.high_ref.fh_ref, bf16[256,256]{1,0:T(8,128)(2,1)} %constant.53.clone.low_ref.fl_ref), custom_call_target="tpu_custom_call" | custom-call | flops 3221225472 | bytes 8388608 | tf_op jit(solution)/shard_map/along_width/pallas_call | solution.py:163
  14.5 62.6 %all_to_all.20.x_ref = f32[32,2,64,128]{3,2,1,0:T(8,128)} all-to-all(f32[32,2,64,128]{3,2,1,0:T(8,128)} %get-tuple-element.8), channel_id=1, replica_groups=mesh['depth_0'=8,'depth_1'=2,'rows'=32] {'rows'}, dimensions={0} | all-to-all | bytes 4194304 | tf_op jit(solution)/shard_map/all_to_all | solution.py:354
  77.1 0.0 copy-start
  77.1 6.0 %all-to-all-start = ((f32[32,2,64,128]{3,2,1,0:T(8,128)}), f32[32,2,64,128]{3,2,1,0:T(8,128)}, u32[]{:S(2)}, u32[]{:S(2)}) async-start(f32[32,2,64,128]{3,2,1,0:T(8,128)} %get-tuple-element.7), calls=%async_computation | async-start | bytes 4194304 | tf_op jit(solution)/shard_map/all_to_all | solution.py:354
  83.1 0.0 reduce-scatter.5.cloned.1.call-start
  83.2 0.0 copy-done
  83.2 0.1 reshape_squeeze.2
  83.4 0.1 convert_element_type.66
  83.4 0.1 copy.31
  84.2 0.2 dynamic-slice_reduce_fusion
  84.4 0.1 convert_bitcast_fusion
  84.5 8.7 %multiply_multiply_fusion.1 = (f32[32,1,64,128]{3,2,1,0:T(8,128)S(1)}, f32[32,1,64,128]{3,2,1,0:T(8,128)S(1)}, f32[32,1,64,128]{3,2,1,0:T(8,128)S(1)}, f32[32,1,64,128]{3,2,1,0:T(8,128)S(1)}) fusion(f32[64]{0:T(128)S(1)} %get-tuple-element.15, f32[32,128]{1,0:T(8,128)S(1)} %copy.31, s32[64]{0:T(128)S(1)} %get-tuple-element.18, s32[32,128]{1,0:T(8,128)S(1)} %fusion.2, ...), kind=kLoop, calls=%fused_computation.5 | loop fusion | flops 7340032 | bytes 4228100 | tf_op jit(solution)/shard_map/mul | solution.py:343
  93.2 1.4 pad_maximum_fusion.1.h_ref
  94.6 4.2 %along_height.4 = f32[32,2,32,128]{3,2,1,0:T(8,128)} custom-call(f32[32,2,64,128]{3,2,1,0:T(8,128)} %all_to_all.20.x_ref, f32[32,2,64,128]{3,2,1,0:T(8,128)} %pad_maximum_fusion.1.h_ref, f32[2,32,128]{2,1,0:T(8,128)} %constant.51.clone.tw_ref.ftw_ref, bf16[256,256]{1,0:T(8,128)(2,1)} %constant.52.clone.high_ref.fh_ref, ...), custom_call_target="tpu_custom_call" | custom-call | flops 1610612736 | bytes 3145728 | tf_op jit(solution)/shard_map/along_height/pallas_call | solution.py:242
  98.8 0.0 reduce-scatter.5.cloned.1.call-update
  98.8 0.2 reduce-scatter.3.cloned.1.call-start
  99.1 1.5 pad_maximum_fusion.h_ref
  100.6 34.3 %all-to-all-done.x_ref = f32[32,2,64,128]{3,2,1,0:T(8,128)} async-done(((f32[32,2,64,128]{3,2,1,0:T(8,128)}), f32[32,2,64,128]{3,2,1,0:T(8,128)}, u32[]{:S(2)}, u32[]{:S(2)}) %all-to-all-start) | async-done | bytes 2097184 | tf_op jit(solution)/shard_map/all_to_all | solution.py:354
  134.9 6.7 %along_height.3 = f32[32,2,64,128]{3,2,1,0:T(8,128)} custom-call(f32[32,2,64,128]{3,2,1,0:T(8,128)} %all-to-all-done.x_ref, f32[32,2,64,128]{3,2,1,0:T(8,128)} %pad_maximum_fusion.h_ref, f32[2,32,128]{2,1,0:T(8,128)} %constant.51.clone.tw_ref.ftw_ref, bf16[256,256]{1,0:T(8,128)(2,1)} %constant.52.clone.high_ref.fh_ref, ...), custom_call_target="tpu_custom_call" | custom-call | flops 3221225472 | bytes 6291456 | tf_op jit(solution)/shard_map/along_height/pallas_call | solution.py:242
  141.6 0.0 reduce-scatter.3.cloned.1.call-update
  141.6 4.2 %along_height.5 = f32[32,2,32,128]{3,2,1,0:T(8,128)} custom-call(f32[32,2,64,128]{3,2,1,0:T(8,128)} %all_to_all.20.x_ref, f32[32,2,64,128]{3,2,1,0:T(8,128)} %pad_maximum_fusion.1.h_ref, f32[2,32,128]{2,1,0:T(8,128)} %constant.51.clone.tw_ref.ftw_ref, bf16[256,256]{1,0:T(8,128)(2,1)} %constant.52.clone.high_ref.fh_ref, ...), custom_call_target="tpu_custom_call" | custom-call | flops 1610612736 | bytes 3145728 | tf_op jit(solution)/shard_map/along_height/pallas_call | solution.py:242
  145.8 46.5 %all_to_all.21 = f32[32,2,32,128]{3,2,1,0:T(8,128)} all-to-all(f32[32,2,32,128]{3,2,1,0:T(8,128)} %along_height.5), channel_id=1, replica_groups=mesh['depth_0'=8,'depth_1'=2,'rows'=32] {'depth_0'}, dimensions={0} | all-to-all | bytes 2097152 | tf_op jit(solution)/shard_map/all_to_all | solution.py:363
  192.4 0.0 reduce-scatter.5.cloned.1.call-done
  192.4 12.0 %reduce-scatter.3.cloned.1.call-done = f32[4,2,64,128]{3,2,1,0:T(8,128)} async-done(((f32[32,2,64,128]{3,2,1,0:T(8,128)}), f32[4,2,64,128]{3,2,1,0:T(8,128)}) %reduce-scatter.3.cloned.1.call-update) | async-done | bytes 262160 | tf_op jit(solution)/shard_map/reduce_scatter | solution.py:360
  204.4 3.5 %flip.1 = f32[64,2,8,128]{3,2,1,0:T(8,128)} custom-call(f32[1,4,2,64,128]{4,3,2,1,0:T(8,128)} %bitcast.11, f32[1,4,2,32,128]{4,3,2,1,0:T(8,128)} %bitcast.13, f32[8,4,2,32,128]{4,3,2,1,0:T(8,128)} %bitcast.10), custom_call_target="tpu_custom_call" | custom-call | tf_op jit(solution)/shard_map/flip/pallas_call | solution.py:281
  207.9 26.4 %all_to_all.22.x_ref = f32[64,2,8,128]{3,2,1,0:T(8,128)} all-to-all(f32[64,2,8,128]{3,2,1,0:T(8,128)} %flip.1), channel_id=1, replica_groups=mesh['depth_0'=8,'depth_1'=2,'rows'=32] {'depth_1','rows'}, dimensions={0} | all-to-all | bytes 1048576 | tf_op jit(solution)/shard_map/all_to_all | solution.py:365
  234.3 2.2 inverse_width.1
  (5 shorter events, 0.1 us)
Async XLA Ops:
  77.1 6.1 %copy-start = (s32[1,2,4096]{2,1,0:T(2,128)S(1)}, s32[1,2,4096]{2,1,0:T(2,128)}, u32[]{:S(2)}) copy-start(s32[1,2,4096]{2,1,0:T(2,128)} %param.29) | copy-start | bytes 98308
  77.1 57.8 %all-to-all-start = ((f32[32,2,64,128]{3,2,1,0:T(8,128)}), f32[32,2,64,128]{3,2,1,0:T(8,128)}, u32[]{:S(2)}, u32[]{:S(2)}) async-start(f32[32,2,64,128]{3,2,1,0:T(8,128)} %get-tuple-element.7), calls=%async_computation | async-start | bytes 4194304 | tf_op jit(solution)/shard_map/all_to_all | solution.py:354
  83.1 109.3 %reduce-scatter.5.cloned.1.call-start = ((), (), s32[]{:S(2)}) async-start(), calls=%async_computation.7 | async-start | bytes 1179648 | tf_op jit(solution)/shard_map/reduce_scatter | solution.py:360
  98.8 105.5 %reduce-scatter.3.cloned.1.call-start = ((), (), s32[]{:S(2)}) async-start(), calls=%async_computation.6 | async-start | bytes 2359296 | tf_op jit(solution)/shard_map/reduce_scatter | solution.py:360
Sparse Core Ops, SparseCore 0:
  99.0 42.9 reduce-scatter.4
  144.8 59.5 reduce-scatter.2

commit v3 on v1

--- a/solution.py
+++ b/solution.py
@@ -15,8 +15,8 @@
 N = 4096
 DEPTH = ("depth_0", "depth_1")
 DEPTH_ROWS = ("depth_0", "depth_1", "rows")
-CHUNKS = (96, 32)
-STARTS = (0, 96)
+CHUNKS = (64, 64)
+STARTS = (0, 64)
 
 
 def block_table(direction, scaling):
@@ -107,7 +107,7 @@
     return dot(high, high_table) + (dot(low, high_table) + dot(high, low_table))
 
 
-WIDTH_ROWS = 16
+WIDTH_ROWS = 32
 WIDTH_STEPS = HIGH // WIDTH_ROWS
 WIDTH_LOWS = LOW // WIDTH_STEPS
 
@@ -232,10 +232,10 @@
 
 
 def along_height(columns, transfer):
+    count = columns.shape[2]
     spec = pl.BlockSpec((LOW, 2, HEIGHT_ROWS, HIGH), lambda i: (0, 0, i, 0))
     table = whole(2 * HIGH, 2 * HIGH)
     forward, backward = block_table(-1.0, 1.0 / 64), block_table(1.0, 1.0 / 64)
-    count = columns.shape[2]
     return pl.pallas_call(
         height_kernel,
         name="along_height",
@@ -262,27 +262,27 @@
     )
 
 
-def flip_kernel(share_ref, parts_ref, out_ref):
+def flip_kernel(x_ref, out_ref):
     for n in range(4):
-        for c in range(2):
-            total = parts_ref[n, c]
-            for source in range(1, 8):
-                total = total + parts_ref[4 * source + n, c]
-            tile = jnp.concatenate([share_ref[n, c], total], axis=0)
-            out_ref[16 * n : 16 * n + 16, c] = tile.T.reshape(16, 8, HIGH)
-
-
-def flip(share, parts):
+        tile = jnp.concatenate([x_ref[n, 0], x_ref[n, 1]], axis=0)
+        out_ref[16 * n : 16 * n + 16] = tile.T.reshape(16, 8, HIGH)
+
+
+def flip(share):
     return pl.pallas_call(
         flip_kernel,
         name="flip",
-        out_shape=jax.ShapeDtypeStruct((64, 2, 8, HIGH), jnp.float32),
-    )(share, parts)
-
-
-def inverse_width_kernel(x_ref, tw_ref, high_ref, low_ref, out_ref, mid_ref, part_ref):
-    total = x_ref[0:LOW] + x_ref[LOW:]
-    rows = jnp.concatenate([total[:, 0], total[:, 1]], axis=-1).reshape(LOW * 8, 2 * HIGH)
+        out_shape=jax.ShapeDtypeStruct((64, 8, HIGH), jnp.float32),
+        cost_estimate=pl.CostEstimate(flops=1 << 18, bytes_accessed=1 << 19, transcendentals=0),
+    )(share)
+
+
+def inverse_width_kernel(
+    first_ref, second_ref, tw_ref, high_ref, low_ref, out_ref, mid_ref, part_ref
+):
+    rows = jnp.concatenate(
+        [ref[0:LOW] + ref[LOW:] for ref in (first_ref, second_ref)], axis=-1
+    ).reshape(LOW * 8, 2 * HIGH)
     mid_ref[...] = product(rows, (high_ref, low_ref)).reshape(LOW, 8, 2 * HIGH)
 
     def load(k):
@@ -298,7 +298,10 @@
 
 
 def inverse_width(pieces, scaling):
-    high, low = block_table(1.0, scaling / 64)
+    high, low = [
+        table.reshape(2, 2, HIGH // 2, 2 * HIGH).swapaxes(0, 1).reshape(table.shape)
+        for table in block_table(1.0, scaling / 64)
+    ]
     return pl.pallas_call(
         inverse_width_kernel,
         name="inverse_width",
@@ -307,7 +310,7 @@
             pltpu.VMEM((LOW, 8, 2 * HIGH), jnp.float32),
             pltpu.VMEM((LOW, 2, 8, HIGH), jnp.float32),
         ],
-    )(pieces, jnp.asarray(twiddles(1.0)), jnp.asarray(high), jnp.asarray(low))
+    )(*pieces, jnp.asarray(twiddles(1.0)), jnp.asarray(high), jnp.asarray(low))
 
 
 def signed(natural):
@@ -334,19 +337,20 @@
 
 def hologram(target, depth_index, band_mask):
     spectra = along_width(target)
-    transfer = [
-        transfer_factors(depth_index, band_mask, lax.axis_index("rows"), start, count)
-        for start, count in zip(STARTS, CHUNKS)
-    ]
-    parts = []
-    for i, (block, start, count) in enumerate(zip(spectra, STARTS, CHUNKS)):
+    transfer = []
+    for start, count in zip(STARTS, CHUNKS):
+        column = lax.axis_index("rows")
+        transfer.append(transfer_factors(depth_index, band_mask, column, start, count))
+    pieces = []
+    for i, block in enumerate(spectra):
         columns = lax.all_to_all(block, "rows", split_axis=0, concat_axis=0, tiled=True)
-        parts.append(along_height(columns, transfer[i]))
-    share = lax.psum_scatter(parts[0], "depth_0", scatter_dimension=0, tiled=True)
-    rest = lax.all_to_all(parts[1], "depth_0", split_axis=0, concat_axis=0, tiled=True)
-    pieces = lax.all_to_all(
-        flip(share, rest), ("depth_1", "rows"), split_axis=0, concat_axis=0, tiled=True
-    )
+        part = along_height(columns, transfer[i])
+        share = lax.psum_scatter(part, "depth_0", scatter_dimension=0, tiled=True)
+        pieces.append(
+            lax.all_to_all(
+                flip(share), ("depth_1", "rows"), split_axis=0, concat_axis=0, tiled=True
+            )
+        )
     return inverse_width(pieces, 1.0 / math.sqrt(lax.axis_size(DEPTH)))
 
 

time: 229 us -> 222 us (0.969)
  blocking collectives: 63.1 us -> 27.6 us
  waiting for transfers between devices: 90 us -> 114 us
  starting transfers between devices: 16.8 us -> 26.6 us
  local copies, waits for them, and re-layouts: 3.13 us -> 0.44 us
    all_to_all x2 -> x1, blocking collectives: 63.1 us -> 27.6 us  [hologram(): lax.all_to_all(flip(share), ('depth_1', 'rows'), split_axis=0, concat_axi...]
    reduce_scatter x1 -> x2, waiting for transfers between devices: 0.01 us -> 30.5 us  [hologram(): share = lax.psum_scatter(part, 'depth_0', scatter_dimension=0, tiled=True)]
    all_to_all x0 -> x1, starting transfers between devices: none -> 9.46 us  [hologram(): lax.all_to_all(flip(share), ('depth_1', 'rows'), split_axis=0, concat_axi...]
    all_to_all x2, waiting for transfers between devices: 90 us -> 83 us  [hologram(): lax.all_to_all(block, 'rows', split_axis=0, concat_axis=0, tiled=True)]
    pallas_call x1, Pallas kernels: 11.2 us -> 7.95 us  [along_width(): pl.pallas_call(width_kernel, name='along_width', grid=(2 * WIDTH_STEPS,),...]
    unnamed x6 -> x4, local copies, waits for them, and re-layouts: 2.7 us -> 0.01 us
    mul x2 -> x1, other arithmetic: 8.82 us -> 8.73 us  [transfer_factors(): jnp.cos(angles) * weights]
  transfers between devices with their start and end apart: 3 -> 5, of which waited for: 2 -> 3; matrix products, arithmetic and copies ran while one was open for 5% -> 6% of each run, Pallas kernels for 2% -> 8%
where the time goes in v3:
time: 222 us; the launch traced here: 221 us
  waiting for transfers between devices  114 us (51%)
  blocking collectives  27.6 us (12%)
  Pallas kernels  27.2 us (12%)
  starting transfers between devices  26.6 us (12%)
  between operations  14.2 us (6%)
  other arithmetic  11.8 us (5%)
    all_to_all x2, waiting for transfers between devices, hologram(): lax.all_to_all(block, 'rows', split_axis=0, concat_axis=0, tiled=True)  83 us
    reduce_scatter x2, waiting for transfers between devices, hologram(): share = lax.psum_scatter(part, 'depth_0', scatter_dimension=0, tiled=True)  30.5 us
    all_to_all x1, blocking collectives, hologram(): lax.all_to_all(flip(share), ('depth_1', 'rows'), split_axis=0, concat_axi...  27.6 us
    all_to_all x2, starting transfers between devices, hologram(): lax.all_to_all(block, 'rows', split_axis=0, concat_axis=0, tiled=True)  16.9 us
    pallas_call x2, Pallas kernels, along_height(): pl.pallas_call(height_kernel, name='along_height', grid=(count // HEIGHT_...  13.5 us
    all_to_all x1, starting transfers between devices, hologram(): lax.all_to_all(flip(share), ('depth_1', 'rows'), split_axis=0, concat_axi...  9.46 us
    mul x1, other arithmetic, transfer_factors(): jnp.cos(angles) * weights  8.73 us
    pallas_call x1, Pallas kernels, along_width(): pl.pallas_call(width_kernel, name='along_width', grid=(2 * WIDTH_STEPS,),...  7.95 us
  transfers between devices with their start and end apart: 5, of which 3 were waited for; matrix products, arithmetic and copies ran while one was open for 6% of the time, Pallas kernels for 8%

profile of v3, /device:TPU:1, one launch (start us, length us, event | category | flops | bytes accessed | tf_op | source)
XLA Modules:
  0.0 221.4 jit_solution(6457480196461747690)
XLA Ops:
  6.5 8.0 %along_width.1 = (f32[32,2,64,128]{3,2,1,0:T(8,128)}, f32[32,2,64,128]{3,2,1,0:T(8,128)}) custom-call(f32[1,2,128,4096]{3,2,1,0:T(8,128)} %x_ref.1, f32[2,32,128]{2,1,0:T(8,128)} %constant.51.clone.tw_ref.ftw_ref, bf16[256,256]{1,0:T(8,128)(2,1)} %constant.52.clone.high_ref.fh_ref, bf16[256,256]{1,0:T(8,128)(2,1)} %constant.53.clone.low_ref.fl_ref), custom_call_target="tpu_custom_call" | custom-call | flops 3221225472 | bytes 8388608 | tf_op jit(solution)/shard_map/along_width/pallas_call | solution.py:162
  14.5 0.0 copy-start.1
  14.5 11.4 %all-to-all-start = ((f32[32,2,64,128]{3,2,1,0:T(8,128)}), f32[32,2,64,128]{3,2,1,0:T(8,128)}, u32[]{:S(2)}, u32[]{:S(2)}) async-start(f32[32,2,64,128]{3,2,1,0:T(8,128)} %get-tuple-element.7), calls=%async_computation | async-start | bytes 4194304 | tf_op jit(solution)/shard_map/all_to_all | solution.py:346
  25.9 0.0 copy-done.1
  26.0 0.1 reshape_squeeze.2
  26.1 0.1 convert_element_type.66
  26.2 0.1 copy.25
  26.9 0.2 dynamic-slice_reduce_fusion
  27.1 0.1 convert_bitcast_fusion
  27.2 8.7 %multiply_multiply_fusion.1 = (f32[32,1,64,128]{3,2,1,0:T(8,128)S(1)}, f32[32,1,64,128]{3,2,1,0:T(8,128)S(1)}, f32[32,1,64,128]{3,2,1,0:T(8,128)S(1)}, f32[32,1,64,128]{3,2,1,0:T(8,128)S(1)}) fusion(f32[64]{0:T(128)S(1)} %get-tuple-element.15, f32[32,128]{1,0:T(8,128)S(1)} %copy.25, s32[64]{0:T(128)S(1)} %get-tuple-element.18, s32[32,128]{1,0:T(8,128)S(1)} %fusion.2, ...), kind=kLoop, calls=%fused_computation.5 | loop fusion | flops 7340032 | bytes 4228100 | tf_op jit(solution)/shard_map/mul | solution.py:335
  35.9 1.5 pad_maximum_fusion.h_ref
  37.4 40.2 %all-to-all-done.x_ref = f32[32,2,64,128]{3,2,1,0:T(8,128)} async-done(((f32[32,2,64,128]{3,2,1,0:T(8,128)}), f32[32,2,64,128]{3,2,1,0:T(8,128)}, u32[]{:S(2)}, u32[]{:S(2)}) %all-to-all-start) | async-done | bytes 2097184 | tf_op jit(solution)/shard_map/all_to_all | solution.py:346
  77.7 5.5 %all-to-all-start.2 = ((f32[32,2,64,128]{3,2,1,0:T(8,128)}), f32[32,2,64,128]{3,2,1,0:T(8,128)}, u32[]{:S(2)}, u32[]{:S(2)}) async-start(f32[32,2,64,128]{3,2,1,0:T(8,128)} %get-tuple-element.8), calls=%async_computation.3 | async-start | bytes 4194304 | tf_op jit(solution)/shard_map/all_to_all | solution.py:346
  83.2 0.2 reduce-scatter.3.cloned.1.call-start
  83.4 6.7 %along_height.2 = f32[32,2,64,128]{3,2,1,0:T(8,128)} custom-call(f32[32,2,64,128]{3,2,1,0:T(8,128)} %all-to-all-done.x_ref, f32[32,2,64,128]{3,2,1,0:T(8,128)} %pad_maximum_fusion.h_ref, f32[2,32,128]{2,1,0:T(8,128)} %constant.51.clone.tw_ref.ftw_ref, bf16[256,256]{1,0:T(8,128)(2,1)} %constant.52.clone.high_ref.fh_ref, ...), custom_call_target="tpu_custom_call" | custom-call | flops 3221225472 | bytes 6291456 | tf_op jit(solution)/shard_map/along_height/pallas_call | solution.py:239
  90.1 0.0 reduce-scatter.3.cloned.1.call-update
  90.2 0.0 reduce-scatter.5.cloned.1.call-start
  90.2 1.5 pad_maximum_fusion.1.h_ref
  91.7 42.8 %all-to-all-done.2.x_ref = f32[32,2,64,128]{3,2,1,0:T(8,128)} async-done(((f32[32,2,64,128]{3,2,1,0:T(8,128)}), f32[32,2,64,128]{3,2,1,0:T(8,128)}, u32[]{:S(2)}, u32[]{:S(2)}) %all-to-all-start.2) | async-done | bytes 2097184 | tf_op jit(solution)/shard_map/all_to_all | solution.py:346
  134.4 6.7 %along_height.3 = f32[32,2,64,128]{3,2,1,0:T(8,128)} custom-call(f32[32,2,64,128]{3,2,1,0:T(8,128)} %all-to-all-done.2.x_ref, f32[32,2,64,128]{3,2,1,0:T(8,128)} %pad_maximum_fusion.1.h_ref, f32[2,32,128]{2,1,0:T(8,128)} %constant.51.clone.tw_ref.ftw_ref, bf16[256,256]{1,0:T(8,128)(2,1)} %constant.52.clone.high_ref.fh_ref, ...), custom_call_target="tpu_custom_call" | custom-call | flops 3221225472 | bytes 6291456 | tf_op jit(solution)/shard_map/along_height/pallas_call | solution.py:239
  141.2 0.0 reduce-scatter.5.cloned.1.call-update
  141.2 0.0 reduce-scatter.3.cloned.1.call-done.x_ref
  141.2 1.8 flip.2
  143.0 9.5 %all-to-all-start.1 = ((f32[64,8,128]{2,1,0:T(8,128)}), f32[64,8,128]{2,1,0:T(8,128)S(1)}, u32[]{:S(2)}, u32[]{:S(2)}) async-start(f32[64,8,128]{2,1,0:T(8,128)} %flip.2), calls=%async_computation.2 | async-start | bytes 524288 | tf_op jit(solution)/shard_map/all_to_all | solution.py:350
  152.5 30.4 %reduce-scatter.5.cloned.1.call-done.x_ref = f32[4,2,64,128]{3,2,1,0:T(8,128)} async-done(((f32[32,2,64,128]{3,2,1,0:T(8,128)}), f32[4,2,64,128]{3,2,1,0:T(8,128)}) %reduce-scatter.5.cloned.1.call-update) | async-done | bytes 262160 | tf_op jit(solution)/shard_map/reduce_scatter | solution.py:348
  182.9 1.8 flip.3
  184.7 0.0 all-to-all-done.1.first_ref
  184.7 0.0 copy-start
  184.7 27.6 %all_to_all.20.second_ref = f32[64,8,128]{2,1,0:T(8,128)} all-to-all(f32[64,8,128]{2,1,0:T(8,128)} %flip.3), channel_id=1, replica_groups=mesh['depth_0'=8,'depth_1'=2,'rows'=32] {'depth_1','rows'}, dimensions={0} | all-to-all | bytes 524288 | tf_op jit(solution)/shard_map/all_to_all | solution.py:350
  212.3 0.0 copy-done
  212.3 2.2 inverse_width.1
  (5 shorter events, 0.1 us)
Async XLA Ops:
  14.5 11.4 %copy-start.1 = (s32[1,2,4096]{2,1,0:T(2,128)S(1)}, s32[1,2,4096]{2,1,0:T(2,128)}, u32[]{:S(2)}) copy-start(s32[1,2,4096]{2,1,0:T(2,128)} %param.23) | copy-start | bytes 98308
  14.5 63.2 %all-to-all-start = ((f32[32,2,64,128]{3,2,1,0:T(8,128)}), f32[32,2,64,128]{3,2,1,0:T(8,128)}, u32[]{:S(2)}, u32[]{:S(2)}) async-start(f32[32,2,64,128]{3,2,1,0:T(8,128)} %get-tuple-element.7), calls=%async_computation | async-start | bytes 4194304 | tf_op jit(solution)/shard_map/all_to_all | solution.py:346
  77.7 56.8 %all-to-all-start.2 = ((f32[32,2,64,128]{3,2,1,0:T(8,128)}), f32[32,2,64,128]{3,2,1,0:T(8,128)}, u32[]{:S(2)}, u32[]{:S(2)}) async-start(f32[32,2,64,128]{3,2,1,0:T(8,128)} %get-tuple-element.8), calls=%async_computation.3 | async-start | bytes 4194304 | tf_op jit(solution)/shard_map/all_to_all | solution.py:346
  83.2 58.1 %reduce-scatter.3.cloned.1.call-start = ((), (), s32[]{:S(2)}) async-start(), calls=%async_computation.6 | async-start | bytes 2359296 | tf_op jit(solution)/shard_map/reduce_scatter | solution.py:348
  90.2 92.8 %reduce-scatter.5.cloned.1.call-start = ((), (), s32[]{:S(2)}) async-start(), calls=%async_computation.7 | async-start | bytes 2359296 | tf_op jit(solution)/shard_map/reduce_scatter | solution.py:348
  143.0 41.7 %all-to-all-start.1 = ((f32[64,8,128]{2,1,0:T(8,128)}), f32[64,8,128]{2,1,0:T(8,128)S(1)}, u32[]{:S(2)}, u32[]{:S(2)}) async-start(f32[64,8,128]{2,1,0:T(8,128)} %flip.2), calls=%async_computation.2 | async-start | bytes 524288 | tf_op jit(solution)/shard_map/all_to_all | solution.py:350
  184.7 27.6 %copy-start = (f32[64,8,128]{2,1,0:T(8,128)}, f32[64,8,128]{2,1,0:T(8,128)S(1)}, u32[]{:S(2)}) copy-start(f32[64,8,128]{2,1,0:T(8,128)S(1)} %all-to-all-done.1.first_ref) | copy-start | bytes 786436
Sparse Core Ops, SparseCore 0:
  90.3 46.0 reduce-scatter.2
  141.3 41.5 reduce-scatter.4

commit v4 on v3

--- a/solution.py
+++ b/solution.py
@@ -112,8 +112,7 @@
 WIDTH_LOWS = LOW // WIDTH_STEPS
 
 
-def width_kernel(x_ref, tw_ref, high_ref, low_ref, *rest):
-    out_refs, (mid_ref, part_ref) = rest[: len(CHUNKS)], rest[len(CHUNKS) :]
+def width_kernel(x_ref, tw_ref, high_ref, low_ref, out_ref, mid_ref, part_ref):
     step = pl.program_id(0)
 
     @pl.when(step < WIDTH_STEPS)
@@ -139,25 +138,21 @@
     def _():
         base = (step - WIDTH_STEPS) * WIDTH_LOWS
         for k in range(WIDTH_LOWS):
-            done = product(mid_ref[base + k], (high_ref, low_ref))
-            for c in range(2):
-                flat = done[:, HIGH * c : HIGH * (c + 1)].T
-                for out_ref, start, count in zip(out_refs, STARTS, CHUNKS):
-                    out_ref[k, c] = flat[start : start + count]
+            flat = product(mid_ref[base + k], (high_ref, low_ref)).T
+            out_ref[k, 0] = flat[: flat.shape[0] // 2]
+            out_ref[k, 1] = flat[flat.shape[0] // 2 :]
 
 
 def whole(*dims):
     return pl.BlockSpec(dims, lambda i: (0,) * len(dims))
 
 
-def along_width(target):
-    high, low = block_table(-1.0, 1.0 / 64)
-    shapes = [jax.ShapeDtypeStruct((LOW, 2, count, HIGH), jnp.float32) for count in CHUNKS]
-    specs = [
-        pl.BlockSpec(
-            (WIDTH_LOWS, 2, count, HIGH), lambda i: (jnp.maximum(i - WIDTH_STEPS, 0), 0, 0, 0)
+def along_width(target, start, count):
+    high, low = [
+        np.concatenate(
+            [table[:, start : start + count], table[:, HIGH + start : HIGH + start + count]], 1
         )
-        for count in CHUNKS
+        for table in block_table(-1.0, 1.0 / 64)
     ]
     return pl.pallas_call(
         width_kernel,
@@ -168,17 +163,19 @@
                 (1, 2, WIDTH_ROWS, N), lambda i: (0, 0, jnp.minimum(i, WIDTH_STEPS - 1), 0)
             ),
             whole(2, LOW, HIGH),
-            whole(2 * HIGH, 2 * HIGH),
-            whole(2 * HIGH, 2 * HIGH),
+            whole(2 * HIGH, 2 * count),
+            whole(2 * HIGH, 2 * count),
         ],
-        out_specs=specs,
-        out_shape=shapes,
+        out_specs=pl.BlockSpec(
+            (WIDTH_LOWS, 2, count, HIGH), lambda i: (jnp.maximum(i - WIDTH_STEPS, 0), 0, 0, 0)
+        ),
+        out_shape=jax.ShapeDtypeStruct((LOW, 2, count, HIGH), jnp.float32),
         scratch_shapes=[
             pltpu.VMEM((LOW, HIGH, 2 * HIGH), jnp.float32),
             pltpu.VMEM((WIDTH_ROWS // 8, LOW, 2, 8, HIGH), jnp.float32),
         ],
         cost_estimate=pl.CostEstimate(
-            flops=6 * N * 512 * 256, bytes_accessed=8 << 20, transcendentals=0
+            flops=6 * N * 512 * 2 * count, bytes_accessed=6 << 20, transcendentals=0
         ),
     )(target, jnp.asarray(twiddles(-1.0)), jnp.asarray(high), jnp.asarray(low))
 
@@ -239,10 +236,11 @@
     return pl.pallas_call(
         height_kernel,
         name="along_height",
+        compiler_params=pltpu.CompilerParams(vmem_limit_bytes=14 << 20),
         grid=(count // HEIGHT_ROWS,),
         in_specs=[spec, spec, whole(2, LOW, HIGH), table, table, whole(2, LOW, HIGH), table, table],
         out_specs=spec,
-        out_shape=jax.ShapeDtypeStruct((LOW, 2, count, HIGH), jnp.float32),
+        out_shape=pltpu.HBM((LOW, 2, count, HIGH), jnp.float32),
         scratch_shapes=[
             pltpu.VMEM((LOW, HEIGHT_ROWS, 2 * HIGH), jnp.float32),
             pltpu.VMEM((HEIGHT_ROWS // 8, LOW, 2, 8, HIGH), jnp.float32),
@@ -305,6 +303,7 @@
     return pl.pallas_call(
         inverse_width_kernel,
         name="inverse_width",
+        compiler_params=pltpu.CompilerParams(vmem_limit_bytes=8 << 20),
         out_shape=jax.ShapeDtypeStruct((2, 8, N), jnp.float32),
         scratch_shapes=[
             pltpu.VMEM((LOW, 8, 2 * HIGH), jnp.float32),
@@ -336,13 +335,13 @@
 
 
 def hologram(target, depth_index, band_mask):
-    spectra = along_width(target)
     transfer = []
     for start, count in zip(STARTS, CHUNKS):
         column = lax.axis_index("rows")
         transfer.append(transfer_factors(depth_index, band_mask, column, start, count))
     pieces = []
-    for i, block in enumerate(spectra):
+    for i, (start, count) in enumerate(zip(STARTS, CHUNKS)):
+        block = along_width(target, start, count)
         columns = lax.all_to_all(block, "rows", split_axis=0, concat_axis=0, tiled=True)
         part = along_height(columns, transfer[i])
         share = lax.psum_scatter(part, "depth_0", scatter_dimension=0, tiled=True)

time: 222 us -> 220 us (level)
  waiting for transfers between devices: 114 us -> 105 us
  Pallas kernels: 27.2 us -> 30.7 us
    all_to_all x2, waiting for transfers between devices: 83 us -> 74.4 us  [hologram(): lax.all_to_all(block, 'rows', split_axis=0, concat_axis=0, tiled=True)]
    pallas_call x1 -> x2, Pallas kernels: 7.95 us -> 14.7 us  [along_width(): pl.pallas_call(width_kernel, name='along_width', grid=(2 * WIDTH_STEPS,),...]
    pallas_call x3, Pallas kernels: 15.7 us -> 12.3 us  [the longest x2 11.3 us: along_height(): pl.pallas_call(height_kernel, name='along_height', compiler_params=pltpu....]
  transfers between devices with their start and end apart: 5 -> 5, of which waited for: 3 -> 3; matrix products, arithmetic and copies ran while one was open for 6% -> 6% of each run, Pallas kernels for 8% -> 10%
where the time goes in v4:
time: 220 us
  waiting for transfers between devices  105 us (48%)
  Pallas kernels  30.7 us (14%)
  blocking collectives  27.7 us (13%)
  starting transfers between devices  26.7 us (12%)
  between operations  14.3 us (6%)
  other arithmetic  13.2 us (6%)
    all_to_all x2, waiting for transfers between devices, hologram(): lax.all_to_all(block, 'rows', split_axis=0, concat_axis=0, tiled=True)  74.4 us
    reduce_scatter x2, waiting for transfers between devices, hologram(): share = lax.psum_scatter(part, 'depth_0', scatter_dimension=0, tiled=True)  30.5 us
    all_to_all x1, blocking collectives, hologram(): lax.all_to_all(flip(share), ('depth_1', 'rows'), split_axis=0, concat_axi...  27.7 us
    all_to_all x2, starting transfers between devices, hologram(): lax.all_to_all(block, 'rows', split_axis=0, concat_axis=0, tiled=True)  16.7 us
    pallas_call x2, Pallas kernels, along_width(): pl.pallas_call(width_kernel, name='along_width', grid=(2 * WIDTH_STEPS,),...  14.7 us
    pallas_call x2, Pallas kernels, along_height(): pl.pallas_call(height_kernel, name='along_height', compiler_params=pltpu....  11.3 us
    mul x1, other arithmetic, transfer_factors(): jnp.cos(angles) * weights  9.95 us
    all_to_all x1, starting transfers between devices, hologram(): lax.all_to_all(flip(share), ('depth_1', 'rows'), split_axis=0, concat_axi...  9.9 us
  transfers between devices with their start and end apart: 5, of which 3 were waited for; matrix products, arithmetic and copies ran while one was open for 6% of the time, Pallas kernels for 10%

profile of v4, /device:TPU:1, one launch (start us, length us, event | category | flops | bytes accessed | tf_op | source)
XLA Modules:
  0.0 219.6 jit_solution(16046392376855554454)
XLA Ops:
  6.5 7.4 %along_width.2 = f32[32,2,64,128]{3,2,1,0:T(8,128)} custom-call(f32[1,2,128,4096]{3,2,1,0:T(8,128)} %x_ref.3, f32[2,32,128]{2,1,0:T(8,128)} %constant.59.clone.tw_ref.ftw_ref, bf16[256,128]{1,0:T(8,128)(2,1)} %constant.60.clone.high_ref, bf16[256,128]{1,0:T(8,128)(2,1)} %constant.61.clone.low_ref), custom_call_target="tpu_custom_call" | custom-call | flops 1610612736 | bytes 6291456 | tf_op jit(solution)/shard_map/along_width/pallas_call | solution.py:157
  13.9 0.0 copy-start.9
  13.9 11.3 %all-to-all-start = ((f32[32,2,64,128]{3,2,1,0:T(8,128)}), f32[32,2,64,128]{3,2,1,0:T(8,128)S(1)}, u32[]{:S(2)}, u32[]{:S(2)}) async-start(f32[32,2,64,128]{3,2,1,0:T(8,128)} %along_width.2), calls=%async_computation | async-start | bytes 4194304 | tf_op jit(solution)/shard_map/all_to_all | solution.py:345
  25.2 0.0 copy-done.9
  25.3 0.1 reshape_squeeze.2
  25.4 0.1 convert_element_type.66
  25.5 0.1 copy.28
  26.2 0.2 dynamic-slice_reduce_fusion
  26.5 7.4 %along_width.3 = f32[32,2,64,128]{3,2,1,0:T(8,128)} custom-call(f32[1,2,128,4096]{3,2,1,0:T(8,128)} %x_ref.3, f32[2,32,128]{2,1,0:T(8,128)} %constant.59.clone.tw_ref.ftw_ref, bf16[256,128]{1,0:T(8,128)(2,1)} %constant.67.clone.high_ref, bf16[256,128]{1,0:T(8,128)(2,1)} %constant.68.clone.low_ref), custom_call_target="tpu_custom_call" | custom-call | flops 1610612736 | bytes 6291456 | tf_op jit(solution)/shard_map/along_width/pallas_call | solution.py:157
  33.8 0.1 convert_bitcast_fusion
  33.9 10.0 %multiply_multiply_fusion.1 = (f32[32,1,64,128]{3,2,1,0:T(8,128)}, f32[32,1,64,128]{3,2,1,0:T(8,128)}, f32[32,1,64,128]{3,2,1,0:T(8,128)S(1)}, f32[32,1,64,128]{3,2,1,0:T(8,128)S(1)}) fusion(f32[64]{0:T(128)S(1)} %get-tuple-element.11, f32[32,128]{1,0:T(8,128)S(1)} %copy.28, s32[64]{0:T(128)S(1)} %get-tuple-element.14, s32[32,128]{1,0:T(8,128)S(1)} %fusion.2, ...), kind=kLoop, calls=%fused_computation.5 | loop fusion | flops 7340032 | bytes 4228100 | tf_op jit(solution)/shard_map/mul | solution.py:334
  43.9 1.5 pad_maximum_fusion.h_ref
  45.3 0.0 copy-start.1
  45.3 0.0 copy-start.4
  45.3 0.0 copy-start.5
  45.3 0.0 copy-start.6
  45.3 0.0 copy-start.7
  45.4 0.0 copy-start.8
  45.4 31.7 %all-to-all-done.x_ref = f32[32,2,64,128]{3,2,1,0:T(8,128)S(1)} async-done(((f32[32,2,64,128]{3,2,1,0:T(8,128)}), f32[32,2,64,128]{3,2,1,0:T(8,128)S(1)}, u32[]{:S(2)}, u32[]{:S(2)}) %all-to-all-start) | async-done | bytes 2097184 | tf_op jit(solution)/shard_map/all_to_all | solution.py:345
  77.0 5.4 %all-to-all-start.2 = ((f32[32,2,64,128]{3,2,1,0:T(8,128)}), f32[32,2,64,128]{3,2,1,0:T(8,128)}, u32[]{:S(2)}, u32[]{:S(2)}) async-start(f32[32,2,64,128]{3,2,1,0:T(8,128)} %along_width.3), calls=%async_computation.3 | async-start | bytes 4194304 | tf_op jit(solution)/shard_map/all_to_all | solution.py:345
  82.4 0.0 reduce-scatter.3.cloned.1.call-start
  82.5 0.0 copy-done.1
  82.5 0.0 copy-done.4
  82.5 0.0 copy-done.5
  82.5 0.0 copy-done.6
  82.5 0.0 copy-done.7
  82.5 0.0 copy-done.8
  82.5 0.0 copy-start
  82.5 1.6 copy-done
  84.1 5.1 %along_height.2 = f32[32,2,64,128]{3,2,1,0:T(8,128)} custom-call(f32[32,2,64,128]{3,2,1,0:T(8,128)S(1)} %all-to-all-done.x_ref, f32[32,2,64,128]{3,2,1,0:T(8,128)S(1)} %copy-done, f32[2,32,128]{2,1,0:T(8,128)S(1)} %copy-done.1, bf16[256,256]{1,0:T(8,128)(2,1)S(1)} %copy-done.5, bf16[256,256]{1,0:T(8,128)(2,1)S(1)} %copy-done.6, f32[2,32,128]{2,1,0:T(8,128)S(1)} %copy-done.4, ...), custom_call_target="tpu_custom_call" | custom-call | flops 3221225472 | bytes 6291456 | tf_op jit(solution)/shard_map/along_height/pallas_call | solution.py:236
  89.3 0.0 reduce-scatter.3.cloned.1.call-update
  89.3 0.0 reduce-scatter.5.cloned.1.call-start
  89.3 1.7 pad_maximum_fusion.1.h_ref
  91.0 42.7 %all-to-all-done.2.x_ref = f32[32,2,64,128]{3,2,1,0:T(8,128)} async-done(((f32[32,2,64,128]{3,2,1,0:T(8,128)}), f32[32,2,64,128]{3,2,1,0:T(8,128)}, u32[]{:S(2)}, u32[]{:S(2)}) %all-to-all-start.2) | async-done | bytes 2097184 | tf_op jit(solution)/shard_map/all_to_all | solution.py:345
  133.7 6.1 %along_height.3 = f32[32,2,64,128]{3,2,1,0:T(8,128)} custom-call(f32[32,2,64,128]{3,2,1,0:T(8,128)} %all-to-all-done.2.x_ref, f32[32,2,64,128]{3,2,1,0:T(8,128)S(1)} %pad_maximum_fusion.1.h_ref, f32[2,32,128]{2,1,0:T(8,128)S(1)} %copy-done.1, bf16[256,256]{1,0:T(8,128)(2,1)S(1)} %copy-done.5, bf16[256,256]{1,0:T(8,128)(2,1)S(1)} %copy-done.6, ...), custom_call_target="tpu_custom_call" | custom-call | flops 3221225472 | bytes 6291456 | tf_op jit(solution)/shard_map/along_height/pallas_call | solution.py:236
  139.9 0.0 copy-start.2
  139.9 0.0 copy-start.3
  139.9 0.0 reduce-scatter.5.cloned.1.call-update
  139.9 0.0 reduce-scatter.3.cloned.1.call-done.x_ref
  140.0 1.9 flip.2
  141.8 9.9 %all-to-all-start.1 = ((f32[64,8,128]{2,1,0:T(8,128)}), f32[64,8,128]{2,1,0:T(8,128)S(1)}, u32[]{:S(2)}, u32[]{:S(2)}) async-start(f32[64,8,128]{2,1,0:T(8,128)} %flip.2), calls=%async_computation.2 | async-start | bytes 524288 | tf_op jit(solution)/shard_map/all_to_all | solution.py:349
  151.7 30.5 %reduce-scatter.5.cloned.1.call-done.x_ref = f32[4,2,64,128]{3,2,1,0:T(8,128)} async-done(((f32[32,2,64,128]{3,2,1,0:T(8,128)}), f32[4,2,64,128]{3,2,1,0:T(8,128)}) %reduce-scatter.5.cloned.1.call-update) | async-done | bytes 262160 | tf_op jit(solution)/shard_map/reduce_scatter | solution.py:347
  182.2 1.8 flip.3
  184.0 0.0 all-to-all-done.1.first_ref
  184.0 27.7 %all_to_all.20.second_ref = f32[64,8,128]{2,1,0:T(8,128)S(1)} all-to-all(f32[64,8,128]{2,1,0:T(8,128)} %flip.3), channel_id=1, replica_groups=mesh['depth_0'=8,'depth_1'=2,'rows'=32] {'depth_1','rows'}, dimensions={0} | all-to-all | bytes 524288 | tf_op jit(solution)/shard_map/all_to_all | solution.py:349
  211.7 0.0 copy-done.2
  211.7 0.0 copy-done.3
  211.7 1.0 inverse_width.1
  (5 shorter events, 0.1 us)
Async XLA Ops:
  13.9 11.4 %copy-start.9 = (s32[1,2,4096]{2,1,0:T(2,128)S(1)}, s32[1,2,4096]{2,1,0:T(2,128)}, u32[]{:S(2)}) copy-start(s32[1,2,4096]{2,1,0:T(2,128)} %param.26) | copy-start | bytes 98308
  13.9 63.1 %all-to-all-start = ((f32[32,2,64,128]{3,2,1,0:T(8,128)}), f32[32,2,64,128]{3,2,1,0:T(8,128)S(1)}, u32[]{:S(2)}, u32[]{:S(2)}) async-start(f32[32,2,64,128]{3,2,1,0:T(8,128)} %along_width.2), calls=%async_computation | async-start | bytes 4194304 | tf_op jit(solution)/shard_map/all_to_all | solution.py:345
  45.3 37.1 %copy-start.1 = (f32[2,32,128]{2,1,0:T(8,128)S(1)}, f32[2,32,128]{2,1,0:T(8,128)}, u32[]{:S(2)}) copy-start(f32[2,32,128]{2,1,0:T(8,128)} %constant.59.clone.tw_ref.ftw_ref) | copy-start | bytes 98308
  45.3 37.1 %copy-start.4 = (f32[2,32,128]{2,1,0:T(8,128)S(1)}, f32[2,32,128]{2,1,0:T(8,128)}, u32[]{:S(2)}) copy-start(f32[2,32,128]{2,1,0:T(8,128)} %constant.64.clone.btw_ref.tw_ref) | copy-start | bytes 98308
  45.3 37.1 %copy-start.5 = (bf16[256,256]{1,0:T(8,128)(2,1)S(1)}, bf16[256,256]{1,0:T(8,128)(2,1)}, u32[]{:S(2)}) copy-start(bf16[256,256]{1,0:T(8,128)(2,1)} %constant.62.clone.fh_ref) | copy-start | bytes 393220
  45.3 37.2 %copy-start.6 = (bf16[256,256]{1,0:T(8,128)(2,1)S(1)}, bf16[256,256]{1,0:T(8,128)(2,1)}, u32[]{:S(2)}) copy-start(bf16[256,256]{1,0:T(8,128)(2,1)} %constant.63.clone.fl_ref) | copy-start | bytes 393220
  45.3 37.2 %copy-start.7 = (bf16[256,256]{1,0:T(8,128)(2,1)S(1)}, bf16[256,256]{1,0:T(8,128)(2,1)}, u32[]{:S(2)}) copy-start(bf16[256,256]{1,0:T(8,128)(2,1)} %constant.65.clone.bh_ref) | copy-start | bytes 393220
  45.4 37.2 %copy-start.8 = (bf16[256,256]{1,0:T(8,128)(2,1)S(1)}, bf16[256,256]{1,0:T(8,128)(2,1)}, u32[]{:S(2)}) copy-start(bf16[256,256]{1,0:T(8,128)(2,1)} %constant.66.clone.bl_ref) | copy-start | bytes 393220
  77.0 56.7 %all-to-all-start.2 = ((f32[32,2,64,128]{3,2,1,0:T(8,128)}), f32[32,2,64,128]{3,2,1,0:T(8,128)}, u32[]{:S(2)}, u32[]{:S(2)}) async-start(f32[32,2,64,128]{3,2,1,0:T(8,128)} %along_width.3), calls=%async_computation.3 | async-start | bytes 4194304 | tf_op jit(solution)/shard_map/all_to_all | solution.py:345
  82.4 57.5 %reduce-scatter.3.cloned.1.call-start = ((), (), s32[]{:S(2)}) async-start(), calls=%async_computation.6 | async-start | bytes 2359296 | tf_op jit(solution)/shard_map/reduce_scatter | solution.py:347
  82.5 1.6 copy-start
  89.3 93.0 %reduce-scatter.5.cloned.1.call-start = ((), (), s32[]{:S(2)}) async-start(), calls=%async_computation.7 | async-start | bytes 2359296 | tf_op jit(solution)/shard_map/reduce_scatter | solution.py:347
  139.9 71.8 %copy-start.2 = (bf16[256,256]{1,0:T(8,128)(2,1)S(1)}, bf16[256,256]{1,0:T(8,128)(2,1)}, u32[]{:S(2)}) copy-start(bf16[256,256]{1,0:T(8,128)(2,1)} %constant.69.clone.high_ref) | copy-start | bytes 393220
  139.9 71.8 %copy-start.3 = (bf16[256,256]{1,0:T(8,128)(2,1)S(1)}, bf16[256,256]{1,0:T(8,128)(2,1)}, u32[]{:S(2)}) copy-start(bf16[256,256]{1,0:T(8,128)(2,1)} %constant.70.clone.low_ref) | copy-start | bytes 393220
  141.8 42.2 %all-to-all-start.1 = ((f32[64,8,128]{2,1,0:T(8,128)}), f32[64,8,128]{2,1,0:T(8,128)S(1)}, u32[]{:S(2)}, u32[]{:S(2)}) async-start(f32[64,8,128]{2,1,0:T(8,128)} %flip.2), calls=%async_computation.2 | async-start | bytes 524288 | tf_op jit(solution)/shard_map/all_to_all | solution.py:349
Sparse Core Ops, SparseCore 0:
  89.4 46.0 reduce-scatter.2
  140.0 42.1 reduce-scatter.4

commit v5 on v4

--- a/solution.py
+++ b/solution.py
@@ -112,7 +112,15 @@
 WIDTH_LOWS = LOW // WIDTH_STEPS
 
 
-def width_kernel(x_ref, tw_ref, high_ref, low_ref, out_ref, mid_ref, part_ref):
+def narrow_product(rows, high_ref, both_ref):
+    high = rows.astype(jnp.bfloat16)
+    low = (rows - high.astype(jnp.float32)).astype(jnp.bfloat16)
+    first = jnp.dot(high, both_ref[...], preferred_element_type=jnp.float32)
+    second = jnp.dot(low, high_ref[...], preferred_element_type=jnp.float32)
+    return first[:, :HIGH] + (first[:, HIGH:] + second)
+
+
+def width_kernel(x_ref, tw_ref, high_ref, both_ref, out_ref, mid_ref, part_ref):
     step = pl.program_id(0)
 
     @pl.when(step < WIDTH_STEPS)
@@ -138,7 +146,7 @@
     def _():
         base = (step - WIDTH_STEPS) * WIDTH_LOWS
         for k in range(WIDTH_LOWS):
-            flat = product(mid_ref[base + k], (high_ref, low_ref)).T
+            flat = narrow_product(mid_ref[base + k], high_ref, both_ref).T
             out_ref[k, 0] = flat[: flat.shape[0] // 2]
             out_ref[k, 1] = flat[flat.shape[0] // 2 :]
 
@@ -163,8 +171,8 @@
                 (1, 2, WIDTH_ROWS, N), lambda i: (0, 0, jnp.minimum(i, WIDTH_STEPS - 1), 0)
             ),
             whole(2, LOW, HIGH),
-            whole(2 * HIGH, 2 * count),
-            whole(2 * HIGH, 2 * count),
+            whole(2 * HIGH, HIGH),
+            whole(2 * HIGH, 2 * HIGH),
         ],
         out_specs=pl.BlockSpec(
             (WIDTH_LOWS, 2, count, HIGH), lambda i: (jnp.maximum(i - WIDTH_STEPS, 0), 0, 0, 0)
@@ -177,7 +185,12 @@
         cost_estimate=pl.CostEstimate(
             flops=6 * N * 512 * 2 * count, bytes_accessed=6 << 20, transcendentals=0
         ),
-    )(target, jnp.asarray(twiddles(-1.0)), jnp.asarray(high), jnp.asarray(low))
+    )(
+        target,
+        jnp.asarray(twiddles(-1.0)),
+        jnp.asarray(high),
+        jnp.asarray(np.concatenate([high, low], 1)),
+    )
 
 
 HEIGHT_ROWS = 16
@@ -270,9 +283,10 @@
     return pl.pallas_call(
         flip_kernel,
         name="flip",
+        compiler_params=pltpu.CompilerParams(vmem_limit_bytes=6 << 20),
         out_shape=jax.ShapeDtypeStruct((64, 8, HIGH), jnp.float32),
         cost_estimate=pl.CostEstimate(flops=1 << 18, bytes_accessed=1 << 19, transcendentals=0),
-    )(share)
+    )(pltpu.with_memory_space_constraint(share, pltpu.HBM))
 
 
 def inverse_width_kernel(

time: 220 us -> 219 us (level)
  no operation moved by 1% of the time
where the time goes in v5:
time: 219 us; the launch traced here: 218 us
  waiting for transfers between devices  105 us (48%)
  Pallas kernels  29.3 us (13%)
  blocking collectives  27.2 us (12%)
  starting transfers between devices  26.7 us (12%)
  between operations  14.3 us (7%)
  other arithmetic  13.2 us (6%)
    all_to_all x2, waiting for transfers between devices, hologram(): lax.all_to_all(block, 'rows', split_axis=0, concat_axis=0, tiled=True)  74.8 us
    reduce_scatter x2, waiting for transfers between devices, hologram(): share = lax.psum_scatter(part, 'depth_0', scatter_dimension=0, tiled=True)  30.5 us
    all_to_all x1, blocking collectives, hologram(): lax.all_to_all(flip(share), ('depth_1', 'rows'), split_axis=0, concat_axi...  27.2 us
    all_to_all x2, starting transfers between devices, hologram(): lax.all_to_all(block, 'rows', split_axis=0, concat_axis=0, tiled=True)  16.7 us
    pallas_call x2, Pallas kernels, along_width(): pl.pallas_call(width_kernel, name='along_width', grid=(2 * WIDTH_STEPS,),...  14 us
    pallas_call x2, Pallas kernels, along_height(): pl.pallas_call(height_kernel, name='along_height', compiler_params=pltpu....  11.3 us
    mul x1, other arithmetic, transfer_factors(): jnp.cos(angles) * weights  9.95 us
    all_to_all x1, starting transfers between devices, hologram(): lax.all_to_all(flip(share), ('depth_1', 'rows'), split_axis=0, concat_axi...  9.89 us
  transfers between devices with their start and end apart: 5, of which 3 were waited for; matrix products, arithmetic and copies ran while one was open for 6% of the time, Pallas kernels for 10%

profile of v5, /device:TPU:1, one launch (start us, length us, event | category | flops | bytes accessed | tf_op | source)
XLA Modules:
  0.0 218.0 jit_solution(16754876934536435269)
XLA Ops:
  6.5 7.0 %along_width.2 = f32[32,2,64,128]{3,2,1,0:T(8,128)} custom-call(f32[1,2,128,4096]{3,2,1,0:T(8,128)} %x_ref.3, f32[2,32,128]{2,1,0:T(8,128)} %constant.59.clone.tw_ref.ftw_ref, bf16[256,128]{1,0:T(8,128)(2,1)} %constant.60.clone.high_ref, bf16[256,256]{1,0:T(8,128)(2,1)} %constant.61.clone.both_ref), custom_call_target="tpu_custom_call" | custom-call | flops 1610612736 | bytes 6291456 | tf_op jit(solution)/shard_map/along_width/pallas_call | solution.py:165
  13.5 0.0 copy-start.9
  13.5 11.3 %all-to-all-start = ((f32[32,2,64,128]{3,2,1,0:T(8,128)}), f32[32,2,64,128]{3,2,1,0:T(8,128)S(1)}, u32[]{:S(2)}, u32[]{:S(2)}) async-start(f32[32,2,64,128]{3,2,1,0:T(8,128)} %along_width.2), calls=%async_computation | async-start | bytes 4194304 | tf_op jit(solution)/shard_map/all_to_all | solution.py:359
  24.9 0.0 copy-done.9
  24.9 0.1 reshape_squeeze.2
  25.1 0.1 convert_element_type.66
  25.1 0.1 copy.28
  25.9 0.2 dynamic-slice_reduce_fusion
  26.1 7.0 %along_width.3 = f32[32,2,64,128]{3,2,1,0:T(8,128)} custom-call(f32[1,2,128,4096]{3,2,1,0:T(8,128)} %x_ref.3, f32[2,32,128]{2,1,0:T(8,128)} %constant.59.clone.tw_ref.ftw_ref, bf16[256,128]{1,0:T(8,128)(2,1)} %constant.67.clone.high_ref, bf16[256,256]{1,0:T(8,128)(2,1)} %constant.68.clone.both_ref), custom_call_target="tpu_custom_call" | custom-call | flops 1610612736 | bytes 6291456 | tf_op jit(solution)/shard_map/along_width/pallas_call | solution.py:165
  33.1 0.1 convert_bitcast_fusion
  33.2 10.0 %multiply_multiply_fusion.1 = (f32[32,1,64,128]{3,2,1,0:T(8,128)}, f32[32,1,64,128]{3,2,1,0:T(8,128)}, f32[32,1,64,128]{3,2,1,0:T(8,128)S(1)}, f32[32,1,64,128]{3,2,1,0:T(8,128)S(1)}) fusion(f32[64]{0:T(128)S(1)} %get-tuple-element.11, f32[32,128]{1,0:T(8,128)S(1)} %copy.28, s32[64]{0:T(128)S(1)} %get-tuple-element.14, s32[32,128]{1,0:T(8,128)S(1)} %fusion.2, ...), kind=kLoop, calls=%fused_computation.5 | loop fusion | flops 7340032 | bytes 4228100 | tf_op jit(solution)/shard_map/mul | solution.py:348
  43.2 1.5 pad_maximum_fusion.h_ref
  44.6 0.0 copy-start.1
  44.6 0.0 copy-start.4
  44.6 0.0 copy-start.5
  44.6 0.0 copy-start.6
  44.6 0.0 copy-start.7
  44.6 0.0 copy-start.8
  44.7 32.0 %all-to-all-done.x_ref = f32[32,2,64,128]{3,2,1,0:T(8,128)S(1)} async-done(((f32[32,2,64,128]{3,2,1,0:T(8,128)}), f32[32,2,64,128]{3,2,1,0:T(8,128)S(1)}, u32[]{:S(2)}, u32[]{:S(2)}) %all-to-all-start) | async-done | bytes 2097184 | tf_op jit(solution)/shard_map/all_to_all | solution.py:359
  76.7 5.4 %all-to-all-start.2 = ((f32[32,2,64,128]{3,2,1,0:T(8,128)}), f32[32,2,64,128]{3,2,1,0:T(8,128)}, u32[]{:S(2)}, u32[]{:S(2)}) async-start(f32[32,2,64,128]{3,2,1,0:T(8,128)} %along_width.3), calls=%async_computation.3 | async-start | bytes 4194304 | tf_op jit(solution)/shard_map/all_to_all | solution.py:359
  82.1 0.0 reduce-scatter.3.cloned.1.call-start
  82.1 0.0 copy-done.1
  82.1 0.0 copy-done.4
  82.1 0.0 copy-done.5
  82.1 0.0 copy-done.6
  82.1 0.0 copy-done.7
  82.2 0.0 copy-done.8
  82.2 0.0 copy-start
  82.2 1.6 copy-done
  83.8 5.1 %along_height.2 = f32[32,2,64,128]{3,2,1,0:T(8,128)} custom-call(f32[32,2,64,128]{3,2,1,0:T(8,128)S(1)} %all-to-all-done.x_ref, f32[32,2,64,128]{3,2,1,0:T(8,128)S(1)} %copy-done, f32[2,32,128]{2,1,0:T(8,128)S(1)} %copy-done.1, bf16[256,256]{1,0:T(8,128)(2,1)S(1)} %copy-done.5, bf16[256,256]{1,0:T(8,128)(2,1)S(1)} %copy-done.6, f32[2,32,128]{2,1,0:T(8,128)S(1)} %copy-done.4, ...), custom_call_target="tpu_custom_call" | custom-call | flops 3221225472 | bytes 6291456 | tf_op jit(solution)/shard_map/along_height/pallas_call | solution.py:249
  88.9 0.0 reduce-scatter.3.cloned.1.call-update
  88.9 0.0 reduce-scatter.5.cloned.1.call-start
  89.0 1.7 pad_maximum_fusion.1.h_ref
  90.7 42.7 %all-to-all-done.2.x_ref = f32[32,2,64,128]{3,2,1,0:T(8,128)} async-done(((f32[32,2,64,128]{3,2,1,0:T(8,128)}), f32[32,2,64,128]{3,2,1,0:T(8,128)}, u32[]{:S(2)}, u32[]{:S(2)}) %all-to-all-start.2) | async-done | bytes 2097184 | tf_op jit(solution)/shard_map/all_to_all | solution.py:359
  133.4 6.2 %along_height.3 = f32[32,2,64,128]{3,2,1,0:T(8,128)} custom-call(f32[32,2,64,128]{3,2,1,0:T(8,128)} %all-to-all-done.2.x_ref, f32[32,2,64,128]{3,2,1,0:T(8,128)S(1)} %pad_maximum_fusion.1.h_ref, f32[2,32,128]{2,1,0:T(8,128)S(1)} %copy-done.1, bf16[256,256]{1,0:T(8,128)(2,1)S(1)} %copy-done.5, bf16[256,256]{1,0:T(8,128)(2,1)S(1)} %copy-done.6, ...), custom_call_target="tpu_custom_call" | custom-call | flops 3221225472 | bytes 6291456 | tf_op jit(solution)/shard_map/along_height/pallas_call | solution.py:249
  139.5 0.0 copy-start.2
  139.6 0.0 copy-start.3
  139.6 0.0 reduce-scatter.5.cloned.1.call-update
  139.6 0.0 reduce-scatter.3.cloned.1.call-done.x_ref
  139.6 1.9 flip.2
  141.5 9.9 %all-to-all-start.1 = ((f32[64,8,128]{2,1,0:T(8,128)}), f32[64,8,128]{2,1,0:T(8,128)S(1)}, u32[]{:S(2)}, u32[]{:S(2)}) async-start(f32[64,8,128]{2,1,0:T(8,128)} %flip.2), calls=%async_computation.2 | async-start | bytes 524288 | tf_op jit(solution)/shard_map/all_to_all | solution.py:363
  151.4 30.5 %reduce-scatter.5.cloned.1.call-done.x_ref = f32[4,2,64,128]{3,2,1,0:T(8,128)} async-done(((f32[32,2,64,128]{3,2,1,0:T(8,128)}), f32[4,2,64,128]{3,2,1,0:T(8,128)}) %reduce-scatter.5.cloned.1.call-update) | async-done | bytes 262160 | tf_op jit(solution)/shard_map/reduce_scatter | solution.py:361
  181.9 1.1 flip.3
  182.9 0.0 all-to-all-done.1.first_ref
  183.0 27.2 %all_to_all.20.second_ref = f32[64,8,128]{2,1,0:T(8,128)S(1)} all-to-all(f32[64,8,128]{2,1,0:T(8,128)S(1)} %flip.3), channel_id=1, replica_groups=mesh['depth_0'=8,'depth_1'=2,'rows'=32] {'depth_1','rows'}, dimensions={0} | all-to-all | bytes 524288 | tf_op jit(solution)/shard_map/all_to_all | solution.py:363
  210.2 0.0 copy-done.2
  210.2 0.0 copy-done.3
  210.2 1.0 inverse_width.1
  (5 shorter events, 0.1 us)
Async XLA Ops:
  13.5 11.4 %copy-start.9 = (s32[1,2,4096]{2,1,0:T(2,128)S(1)}, s32[1,2,4096]{2,1,0:T(2,128)}, u32[]{:S(2)}) copy-start(s32[1,2,4096]{2,1,0:T(2,128)} %param.26) | copy-start | bytes 98308
  13.5 63.1 %all-to-all-start = ((f32[32,2,64,128]{3,2,1,0:T(8,128)}), f32[32,2,64,128]{3,2,1,0:T(8,128)S(1)}, u32[]{:S(2)}, u32[]{:S(2)}) async-start(f32[32,2,64,128]{3,2,1,0:T(8,128)} %along_width.2), calls=%async_computation | async-start | bytes 4194304 | tf_op jit(solution)/shard_map/all_to_all | solution.py:359
  44.6 37.5 %copy-start.1 = (f32[2,32,128]{2,1,0:T(8,128)S(1)}, f32[2,32,128]{2,1,0:T(8,128)}, u32[]{:S(2)}) copy-start(f32[2,32,128]{2,1,0:T(8,128)} %constant.59.clone.tw_ref.ftw_ref) | copy-start | bytes 98308
  44.6 37.5 %copy-start.4 = (f32[2,32,128]{2,1,0:T(8,128)S(1)}, f32[2,32,128]{2,1,0:T(8,128)}, u32[]{:S(2)}) copy-start(f32[2,32,128]{2,1,0:T(8,128)} %constant.64.clone.btw_ref.tw_ref) | copy-start | bytes 98308
  44.6 37.5 %copy-start.5 = (bf16[256,256]{1,0:T(8,128)(2,1)S(1)}, bf16[256,256]{1,0:T(8,128)(2,1)}, u32[]{:S(2)}) copy-start(bf16[256,256]{1,0:T(8,128)(2,1)} %constant.62.clone.fh_ref) | copy-start | bytes 393220
  44.6 37.5 %copy-start.6 = (bf16[256,256]{1,0:T(8,128)(2,1)S(1)}, bf16[256,256]{1,0:T(8,128)(2,1)}, u32[]{:S(2)}) copy-start(bf16[256,256]{1,0:T(8,128)(2,1)} %constant.63.clone.fl_ref) | copy-start | bytes 393220
  44.6 37.5 %copy-start.7 = (bf16[256,256]{1,0:T(8,128)(2,1)S(1)}, bf16[256,256]{1,0:T(8,128)(2,1)}, u32[]{:S(2)}) copy-start(bf16[256,256]{1,0:T(8,128)(2,1)} %constant.65.clone.bh_ref) | copy-start | bytes 393220
  44.6 37.5 %copy-start.8 = (bf16[256,256]{1,0:T(8,128)(2,1)S(1)}, bf16[256,256]{1,0:T(8,128)(2,1)}, u32[]{:S(2)}) copy-start(bf16[256,256]{1,0:T(8,128)(2,1)} %constant.66.clone.bl_ref) | copy-start | bytes 393220
  76.7 56.7 %all-to-all-start.2 = ((f32[32,2,64,128]{3,2,1,0:T(8,128)}), f32[32,2,64,128]{3,2,1,0:T(8,128)}, u32[]{:S(2)}, u32[]{:S(2)}) async-start(f32[32,2,64,128]{3,2,1,0:T(8,128)} %along_width.3), calls=%async_computation.3 | async-start | bytes 4194304 | tf_op jit(solution)/shard_map/all_to_all | solution.py:359
  82.1 57.5 %reduce-scatter.3.cloned.1.call-start = ((), (), s32[]{:S(2)}) async-start(), calls=%async_computation.6 | async-start | bytes 2359296 | tf_op jit(solution)/shard_map/reduce_scatter | solution.py:361
  82.2 1.6 copy-start
  88.9 92.9 %reduce-scatter.5.cloned.1.call-start = ((), (), s32[]{:S(2)}) async-start(), calls=%async_computation.7 | async-start | bytes 2359296 | tf_op jit(solution)/shard_map/reduce_scatter | solution.py:361
  139.5 70.6 %copy-start.2 = (bf16[256,256]{1,0:T(8,128)(2,1)S(1)}, bf16[256,256]{1,0:T(8,128)(2,1)}, u32[]{:S(2)}) copy-start(bf16[256,256]{1,0:T(8,128)(2,1)} %constant.69.clone.high_ref) | copy-start | bytes 393220
  139.6 70.6 %copy-start.3 = (bf16[256,256]{1,0:T(8,128)(2,1)S(1)}, bf16[256,256]{1,0:T(8,128)(2,1)}, u32[]{:S(2)}) copy-start(bf16[256,256]{1,0:T(8,128)(2,1)} %constant.70.clone.low_ref) | copy-start | bytes 393220
  141.5 41.5 %all-to-all-start.1 = ((f32[64,8,128]{2,1,0:T(8,128)}), f32[64,8,128]{2,1,0:T(8,128)S(1)}, u32[]{:S(2)}, u32[]{:S(2)}) async-start(f32[64,8,128]{2,1,0:T(8,128)} %flip.2), calls=%async_computation.2 | async-start | bytes 524288 | tf_op jit(solution)/shard_map/all_to_all | solution.py:363
Sparse Core Ops, SparseCore 0:
  89.0 46.0 reduce-scatter.2
  139.7 42.1 reduce-scatter.4

commit v6 on v5

--- a/solution.py
+++ b/solution.py
@@ -193,7 +193,7 @@
     )
 
 
-HEIGHT_ROWS = 16
+HEIGHT_ROWS = 32
 
 
 def height_kernel(x_ref, h_ref, ftw_ref, fh_ref, fl_ref, btw_ref, bh_ref, bl_ref,
@@ -352,7 +352,10 @@
     transfer = []
     for start, count in zip(STARTS, CHUNKS):
         column = lax.axis_index("rows")
-        transfer.append(transfer_factors(depth_index, band_mask, column, start, count))
+        factors = transfer_factors(depth_index, band_mask, column, start, count)
+        if start == 0:
+            factors = pltpu.with_memory_space_constraint(factors, pltpu.HBM)
+        transfer.append(factors)
     pieces = []
     for i, (start, count) in enumerate(zip(STARTS, CHUNKS)):
         block = along_width(target, start, count)

time: 219 us -> 218 us (level)
  no operation moved by 1% of the time
where the time goes in v6:
time: 218 us; the launch traced here: 217 us
  waiting for transfers between devices  106 us (49%)
  Pallas kernels  29.7 us (14%)
  blocking collectives  27.1 us (12%)
  starting transfers between devices  26.2 us (12%)
  between operations  14.3 us (7%)
  other arithmetic  13.3 us (6%)
    all_to_all x2, waiting for transfers between devices, hologram(): lax.all_to_all(block, 'rows', split_axis=0, concat_axis=0, tiled=True)  75.5 us
    reduce_scatter x2, waiting for transfers between devices, hologram(): share = lax.psum_scatter(part, 'depth_0', scatter_dimension=0, tiled=True)  30.4 us
    all_to_all x1, blocking collectives, hologram(): lax.all_to_all(flip(share), ('depth_1', 'rows'), split_axis=0, concat_axi...  27.1 us
    all_to_all x2, starting transfers between devices, hologram(): lax.all_to_all(block, 'rows', split_axis=0, concat_axis=0, tiled=True)  16.7 us
    pallas_call x2, Pallas kernels, along_width(): pl.pallas_call(width_kernel, name='along_width', grid=(2 * WIDTH_STEPS,),...  14 us
    pallas_call x2, Pallas kernels, along_height(): pl.pallas_call(height_kernel, name='along_height', compiler_params=pltpu....  11.8 us
    mul x1, other arithmetic, transfer_factors(): jnp.cos(angles) * weights  9.95 us
    all_to_all x1, starting transfers between devices, hologram(): lax.all_to_all(flip(share), ('depth_1', 'rows'), split_axis=0, concat_axi...  9.39 us
  transfers between devices with their start and end apart: 5, of which 3 were waited for; matrix products, arithmetic and copies ran while one was open for 6% of the time, Pallas kernels for 10%

profile of v6, /device:TPU:1, one launch (start us, length us, event | category | flops | bytes accessed | tf_op | source)
XLA Modules:
  0.0 217.1 jit_solution(4188437055096633698)
XLA Ops:
  6.5 7.0 %along_width.2 = f32[32,2,64,128]{3,2,1,0:T(8,128)} custom-call(f32[1,2,128,4096]{3,2,1,0:T(8,128)} %x_ref.3, f32[2,32,128]{2,1,0:T(8,128)} %constant.59.clone.tw_ref.ftw_ref, bf16[256,128]{1,0:T(8,128)(2,1)} %constant.60.clone.high_ref, bf16[256,256]{1,0:T(8,128)(2,1)} %constant.61.clone.both_ref), custom_call_target="tpu_custom_call" | custom-call | flops 1610612736 | bytes 6291456 | tf_op jit(solution)/shard_map/along_width/pallas_call | solution.py:165
  13.5 0.0 copy-start.8
  13.5 11.3 %all-to-all-start = ((f32[32,2,64,128]{3,2,1,0:T(8,128)}), f32[32,2,64,128]{3,2,1,0:T(8,128)S(1)}, u32[]{:S(2)}, u32[]{:S(2)}) async-start(f32[32,2,64,128]{3,2,1,0:T(8,128)} %along_width.2), calls=%async_computation | async-start | bytes 4194304 | tf_op jit(solution)/shard_map/all_to_all | solution.py:362
  24.9 0.0 copy-done.8
  25.0 0.1 reshape_squeeze.2
  25.1 0.1 convert_element_type.66
  25.2 0.1 copy.28
  25.9 0.2 dynamic-slice_reduce_fusion
  26.1 7.0 %along_width.3 = f32[32,2,64,128]{3,2,1,0:T(8,128)} custom-call(f32[1,2,128,4096]{3,2,1,0:T(8,128)} %x_ref.3, f32[2,32,128]{2,1,0:T(8,128)} %constant.59.clone.tw_ref.ftw_ref, bf16[256,128]{1,0:T(8,128)(2,1)} %constant.67.clone.high_ref, bf16[256,256]{1,0:T(8,128)(2,1)} %constant.68.clone.both_ref), custom_call_target="tpu_custom_call" | custom-call | flops 1610612736 | bytes 6291456 | tf_op jit(solution)/shard_map/along_width/pallas_call | solution.py:165
  33.1 0.1 convert_bitcast_fusion
  33.2 10.0 %multiply_multiply_fusion.1 = (f32[32,1,64,128]{3,2,1,0:T(8,128)}, f32[32,1,64,128]{3,2,1,0:T(8,128)}, f32[32,1,64,128]{3,2,1,0:T(8,128)S(1)}, f32[32,1,64,128]{3,2,1,0:T(8,128)S(1)}) fusion(f32[64]{0:T(128)S(1)} %get-tuple-element.11, f32[32,128]{1,0:T(8,128)S(1)} %copy.28, s32[64]{0:T(128)S(1)} %get-tuple-element.14, s32[32,128]{1,0:T(8,128)S(1)} %fusion.2, ...), kind=kLoop, calls=%fused_computation.5 | loop fusion | flops 7340032 | bytes 4228100 | tf_op jit(solution)/shard_map/mul | solution.py:348
  43.2 1.5 pad_maximum_fusion.h_ref
  44.6 0.0 copy-start
  44.6 0.0 copy-start.3
  44.6 0.0 copy-start.4
  44.6 0.0 copy-start.5
  44.6 0.0 copy-start.6
  44.7 0.0 copy-start.7
  44.7 32.0 %all-to-all-done.x_ref = f32[32,2,64,128]{3,2,1,0:T(8,128)S(1)} async-done(((f32[32,2,64,128]{3,2,1,0:T(8,128)}), f32[32,2,64,128]{3,2,1,0:T(8,128)S(1)}, u32[]{:S(2)}, u32[]{:S(2)}) %all-to-all-start) | async-done | bytes 2097184 | tf_op jit(solution)/shard_map/all_to_all | solution.py:362
  76.7 5.4 %all-to-all-start.2 = ((f32[32,2,64,128]{3,2,1,0:T(8,128)}), f32[32,2,64,128]{3,2,1,0:T(8,128)}, u32[]{:S(2)}, u32[]{:S(2)}) async-start(f32[32,2,64,128]{3,2,1,0:T(8,128)} %along_width.3), calls=%async_computation.3 | async-start | bytes 4194304 | tf_op jit(solution)/shard_map/all_to_all | solution.py:362
  82.1 0.0 reduce-scatter.3.cloned.1.call-start
  82.1 0.0 copy-done
  82.1 0.0 copy-done.3
  82.1 0.0 copy-done.4
  82.1 0.0 copy-done.5
  82.2 0.0 copy-done.6
  82.2 0.0 copy-done.7
  82.2 5.9 %along_height.2 = f32[32,2,64,128]{3,2,1,0:T(8,128)} custom-call(f32[32,2,64,128]{3,2,1,0:T(8,128)S(1)} %all-to-all-done.x_ref, f32[32,2,64,128]{3,2,1,0:T(8,128)} %pad_maximum_fusion.h_ref, f32[2,32,128]{2,1,0:T(8,128)S(1)} %copy-done, bf16[256,256]{1,0:T(8,128)(2,1)S(1)} %copy-done.4, bf16[256,256]{1,0:T(8,128)(2,1)S(1)} %copy-done.5, ...), custom_call_target="tpu_custom_call" | custom-call | flops 3221225472 | bytes 6291456 | tf_op jit(solution)/shard_map/along_height/pallas_call | solution.py:249
  88.1 0.0 reduce-scatter.3.cloned.1.call-update
  88.1 0.0 reduce-scatter.5.cloned.1.call-start
  88.2 1.7 pad_maximum_fusion.1.h_ref
  89.9 43.5 %all-to-all-done.2.x_ref = f32[32,2,64,128]{3,2,1,0:T(8,128)} async-done(((f32[32,2,64,128]{3,2,1,0:T(8,128)}), f32[32,2,64,128]{3,2,1,0:T(8,128)}, u32[]{:S(2)}, u32[]{:S(2)}) %all-to-all-start.2) | async-done | bytes 2097184 | tf_op jit(solution)/shard_map/all_to_all | solution.py:362
  133.4 5.8 %along_height.3 = f32[32,2,64,128]{3,2,1,0:T(8,128)} custom-call(f32[32,2,64,128]{3,2,1,0:T(8,128)} %all-to-all-done.2.x_ref, f32[32,2,64,128]{3,2,1,0:T(8,128)S(1)} %pad_maximum_fusion.1.h_ref, f32[2,32,128]{2,1,0:T(8,128)S(1)} %copy-done, bf16[256,256]{1,0:T(8,128)(2,1)S(1)} %copy-done.4, bf16[256,256]{1,0:T(8,128)(2,1)S(1)} %copy-done.5, ...), custom_call_target="tpu_custom_call" | custom-call | flops 3221225472 | bytes 6291456 | tf_op jit(solution)/shard_map/along_height/pallas_call | solution.py:249
  139.2 0.0 copy-start.1
  139.2 0.0 copy-start.2
  139.2 0.0 reduce-scatter.5.cloned.1.call-update
  139.3 0.0 reduce-scatter.3.cloned.1.call-done.x_ref
  139.3 1.9 flip.2
  141.1 9.4 %all-to-all-start.1 = ((f32[64,8,128]{2,1,0:T(8,128)}), f32[64,8,128]{2,1,0:T(8,128)S(1)}, u32[]{:S(2)}, u32[]{:S(2)}) async-start(f32[64,8,128]{2,1,0:T(8,128)} %flip.2), calls=%async_computation.2 | async-start | bytes 524288 | tf_op jit(solution)/shard_map/all_to_all | solution.py:366
  150.5 30.4 %reduce-scatter.5.cloned.1.call-done.x_ref = f32[4,2,64,128]{3,2,1,0:T(8,128)} async-done(((f32[32,2,64,128]{3,2,1,0:T(8,128)}), f32[4,2,64,128]{3,2,1,0:T(8,128)}) %reduce-scatter.5.cloned.1.call-update) | async-done | bytes 262160 | tf_op jit(solution)/shard_map/reduce_scatter | solution.py:364
  180.9 1.1 flip.3
  182.0 0.0 all-to-all-done.1.first_ref
  182.0 27.1 %all_to_all.20.second_ref = f32[64,8,128]{2,1,0:T(8,128)S(1)} all-to-all(f32[64,8,128]{2,1,0:T(8,128)S(1)} %flip.3), channel_id=1, replica_groups=mesh['depth_0'=8,'depth_1'=2,'rows'=32] {'depth_1','rows'}, dimensions={0} | all-to-all | bytes 524288 | tf_op jit(solution)/shard_map/all_to_all | solution.py:366
  209.2 0.0 copy-done.1
  209.2 0.0 copy-done.2
  209.2 1.0 inverse_width.1
  (5 shorter events, 0.1 us)
Async XLA Ops:
  13.5 11.4 %copy-start.8 = (s32[1,2,4096]{2,1,0:T(2,128)S(1)}, s32[1,2,4096]{2,1,0:T(2,128)}, u32[]{:S(2)}) copy-start(s32[1,2,4096]{2,1,0:T(2,128)} %param.26) | copy-start | bytes 98308
  13.5 63.1 %all-to-all-start = ((f32[32,2,64,128]{3,2,1,0:T(8,128)}), f32[32,2,64,128]{3,2,1,0:T(8,128)S(1)}, u32[]{:S(2)}, u32[]{:S(2)}) async-start(f32[32,2,64,128]{3,2,1,0:T(8,128)} %along_width.2), calls=%async_computation | async-start | bytes 4194304 | tf_op jit(solution)/shard_map/all_to_all | solution.py:362
  44.6 37.5 %copy-start = (f32[2,32,128]{2,1,0:T(8,128)S(1)}, f32[2,32,128]{2,1,0:T(8,128)}, u32[]{:S(2)}) copy-start(f32[2,32,128]{2,1,0:T(8,128)} %constant.59.clone.tw_ref.ftw_ref) | copy-start | bytes 98308
  44.6 37.5 %copy-start.3 = (f32[2,32,128]{2,1,0:T(8,128)S(1)}, f32[2,32,128]{2,1,0:T(8,128)}, u32[]{:S(2)}) copy-start(f32[2,32,128]{2,1,0:T(8,128)} %constant.64.clone.btw_ref.tw_ref) | copy-start | bytes 98308
  44.6 37.5 %copy-start.4 = (bf16[256,256]{1,0:T(8,128)(2,1)S(1)}, bf16[256,256]{1,0:T(8,128)(2,1)}, u32[]{:S(2)}) copy-start(bf16[256,256]{1,0:T(8,128)(2,1)} %constant.62.clone.fh_ref) | copy-start | bytes 393220
  44.6 37.5 %copy-start.5 = (bf16[256,256]{1,0:T(8,128)(2,1)S(1)}, bf16[256,256]{1,0:T(8,128)(2,1)}, u32[]{:S(2)}) copy-start(bf16[256,256]{1,0:T(8,128)(2,1)} %constant.63.clone.fl_ref) | copy-start | bytes 393220
  44.6 37.5 %copy-start.6 = (bf16[256,256]{1,0:T(8,128)(2,1)S(1)}, bf16[256,256]{1,0:T(8,128)(2,1)}, u32[]{:S(2)}) copy-start(bf16[256,256]{1,0:T(8,128)(2,1)} %constant.65.clone.bh_ref) | copy-start | bytes 393220
  44.7 37.5 %copy-start.7 = (bf16[256,256]{1,0:T(8,128)(2,1)S(1)}, bf16[256,256]{1,0:T(8,128)(2,1)}, u32[]{:S(2)}) copy-start(bf16[256,256]{1,0:T(8,128)(2,1)} %constant.66.clone.bl_ref) | copy-start | bytes 393220
  76.7 56.7 %all-to-all-start.2 = ((f32[32,2,64,128]{3,2,1,0:T(8,128)}), f32[32,2,64,128]{3,2,1,0:T(8,128)}, u32[]{:S(2)}, u32[]{:S(2)}) async-start(f32[32,2,64,128]{3,2,1,0:T(8,128)} %along_width.3), calls=%async_computation.3 | async-start | bytes 4194304 | tf_op jit(solution)/shard_map/all_to_all | solution.py:362
  82.1 57.2 %reduce-scatter.3.cloned.1.call-start = ((), (), s32[]{:S(2)}) async-start(), calls=%async_computation.6 | async-start | bytes 2359296 | tf_op jit(solution)/shard_map/reduce_scatter | solution.py:364
  88.1 92.8 %reduce-scatter.5.cloned.1.call-start = ((), (), s32[]{:S(2)}) async-start(), calls=%async_computation.7 | async-start | bytes 2359296 | tf_op jit(solution)/shard_map/reduce_scatter | solution.py:364
  139.2 69.9 %copy-start.1 = (bf16[256,256]{1,0:T(8,128)(2,1)S(1)}, bf16[256,256]{1,0:T(8,128)(2,1)}, u32[]{:S(2)}) copy-start(bf16[256,256]{1,0:T(8,128)(2,1)} %constant.69.clone.high_ref) | copy-start | bytes 393220
  139.2 69.9 %copy-start.2 = (bf16[256,256]{1,0:T(8,128)(2,1)S(1)}, bf16[256,256]{1,0:T(8,128)(2,1)}, u32[]{:S(2)}) copy-start(bf16[256,256]{1,0:T(8,128)(2,1)} %constant.70.clone.low_ref) | copy-start | bytes 393220
  141.1 40.9 %all-to-all-start.1 = ((f32[64,8,128]{2,1,0:T(8,128)}), f32[64,8,128]{2,1,0:T(8,128)S(1)}, u32[]{:S(2)}, u32[]{:S(2)}) async-start(f32[64,8,128]{2,1,0:T(8,128)} %flip.2), calls=%async_computation.2 | async-start | bytes 524288 | tf_op jit(solution)/shard_map/all_to_all | solution.py:366
Sparse Core Ops, SparseCore 0:
  88.2 46.0 reduce-scatter.2
  139.4 41.5 reduce-scatter.4
